TPU v7x, 128 devices: a whole 4x4x4 slice. The times are simulated.
128 devices in a mesh: dp: 1, vp: 128 (over z, y, x, core).
Axes of the slice: x: 4, y: 4, z: 4, core: 2. Of those that a mesh axis runs over, the one named last changes fastest.
Arguments:
- hidden: bfloat16 [4096, 1024], P(('dp', 'vp'))
- labels: int32 [4096], P(('dp', 'vp'))
- loss_weight: float32 [4096], P(('dp', 'vp'))
- norm_gain: float32 [1024], replicated
- w_unembed: bfloat16 [1024, 50432], P(None, 'vp')
Outputs:
- output 1: float32 [1], P('dp')
- output 2: bfloat16 [4096, 1024], P(('dp', 'vp'))
- output 3: float32 [1024, 50432], P('dp', 'vp')
- output 4: float32 [1024], P('dp')
All inputs are finite; a program needn't handle non-finite values.
Results may differ from a plain program's by a relative error of at most 0.001.
Values are sent between devices in bfloat16 or wider.
A program may use at most 1 GiB of HBM per device.

v0:
```python
import jax
import jax.numpy as jnp
from jax import lax
from jax.sharding import PartitionSpec as P

NORM_EPS = 1e-5
PAD_COLS = 128


def solution(mesh):
    group_size = mesh.shape["vp"]

    def local_step(hidden, labels, loss_weight, norm_gain, w_local):
        vocab_local = w_local.shape[1]
        vocab_real = vocab_local * group_size - PAD_COLS
        x_float = hidden.astype(jnp.float32)
        inv_rms = lax.rsqrt(jnp.mean(x_float * x_float, axis=-1, keepdims=True) + NORM_EPS)
        x_norm = x_float * inv_rms
        normed = (x_norm * norm_gain).astype(jnp.bfloat16)
        normed_all = lax.all_gather(normed, "vp", axis=0, tiled=True)
        labels_all = lax.all_gather(labels, "vp", axis=0, tiled=True)
        weights_all = lax.all_gather(loss_weight, "vp", axis=0, tiled=True)
        col_ids = lax.axis_index("vp") * vocab_local + lax.broadcasted_iota(jnp.int32, (1, vocab_local), 1)
        logits = jnp.dot(normed_all, w_local, preferred_element_type=jnp.float32)
        logits = jnp.where(col_ids < vocab_real, logits, -jnp.inf)
        is_target = col_ids == labels_all[:, None]
        row_max = lax.pmax(jnp.max(logits, axis=1), "vp")
        shifted = jnp.exp(logits - row_max[:, None])
        sum_exp = lax.psum(jnp.sum(shifted, axis=1), "vp")
        target = lax.psum(jnp.sum(jnp.where(is_target, logits, 0.0), axis=1), "vp")
        log_norm = row_max + jnp.log(sum_exp)
        tok_scale = weights_all / jnp.sum(weights_all)
        mean_loss = jnp.sum(tok_scale * (log_norm - target)).reshape(1)
        prob_all = shifted / sum_exp[:, None]
        d_logits = ((prob_all - jnp.where(is_target, 1.0, 0.0)) * tok_scale[:, None]).astype(jnp.bfloat16)
        d_unembed = lax.dot_general(normed_all, d_logits, (((0,), (0,)), ((), ())), preferred_element_type=jnp.float32)
        d_part = lax.dot_general(d_logits, w_local, (((1,), (1,)), ((), ())), preferred_element_type=jnp.float32)
        d_normed = lax.psum_scatter(d_part, "vp", scatter_dimension=0, tiled=True)
        grad_hat = d_normed * norm_gain
        d_input = inv_rms * (grad_hat - x_norm * jnp.mean(grad_hat * x_norm, axis=-1, keepdims=True))
        d_norm_gain = lax.psum(jnp.sum(d_normed * x_norm, axis=0), "vp")
        return mean_loss, d_input.astype(jnp.bfloat16), d_unembed, d_norm_gain

    return jax.shard_map(
        local_step,
        mesh=mesh,
        in_specs=(P(("dp", "vp"), None), P(("dp", "vp")), P(("dp", "vp")), P(None), P(None, "vp")),
        out_specs=(P("dp"), P(("dp", "vp"), None), P("dp", "vp"), P("dp")),
        check_vma=False,
    )
```

profile of v0, /device:TPU:0, one launch (start us, length us, event | category | flops | bytes accessed | tf_op | source)
XLA Modules:
  0.0 982.2 jit_solution(4666719551822135322)
XLA Ops:
  7.2 0.0 copy-start
  7.2 0.0 all-gather.2.cloned.1.call-start
  7.2 1.0 fusion.15
  8.3 1.6 fusion.9
  9.8 0.0 all-gather.2.cloned.1.call-update
  9.8 0.0 reduce-scatter.2.cloned.1.call-start
  9.9 0.9 dynamic-update-slice
  10.8 0.9 dynamic-update-slice.1
  11.6 69.2 %all-reduce.1 = s32[4096]{0:T(1024)S(1)} all-reduce(s32[4096]{0:T(1024)S(1)} %dynamic-update-slice.1), channel_id=1, replica_groups=mesh['dp'=1,'vp'=128] {'vp'}, use_global_device_ids=true, to_apply=%add.1 | all-reduce | flops 4096 | bytes 32768
  80.8 3.3 all-gather.2.cloned.1.call-done
  84.1 10.8 %fusion.20 = (f32[4096]{0:T(1024)S(1)}, f32[4096,394]{0,1:T(8,128)}) fusion(bf16[4096,1024]{1,0:T(8,128)(2,1)} %all-gather.2.cloned.1.call-done, bf16[1024,394]{0,1:T(8,128)(2,1)S(1)} %copy-done, pred[394]{0:T(512)(128)(4,1)S(1)} %broadcast_compare_fusion), kind=kOutput, calls=%fused_computation.30 | convolution fusion | flops 3308335104 | bytes 15667594 | tf_op jit(solution)/shard_map/dot_general | solution.py:24
  94.9 63.3 %pmax.7 = f32[4096]{0:T(1024)S(1)} all-reduce(f32[4096]{0:T(1024)S(1)} %get-tuple-element.12), channel_id=1, replica_groups=mesh['dp'=1,'vp'=128] {'vp'}, use_global_device_ids=true, to_apply=%region_3.4 | all-reduce | flops 4096 | bytes 32768 | tf_op jit(solution)/shard_map/pmax | solution.py:27
  158.2 3.8 fusion.4
  162.0 64.2 %all-reduce.3 = (f32[4096]{0:T(1024)S(1)}, f32[4096]{0:T(1024)S(1)}) all-reduce(f32[4096]{0:T(1024)S(1)} %dynamic-update-slice, f32[4096]{0:T(1024)S(1)} %get-tuple-element.4), channel_id=1, replica_groups=mesh['dp'=1,'vp'=128] {'vp'}, use_global_device_ids=true, to_apply=%add | all-reduce | flops 8192 | bytes 65536
  226.2 0.6 reduce_sum.63
  226.8 0.6 broadcast_divide_fusion
  227.4 12.5 %fusion.18 = f32[4096,1024]{1,0:T(8,128)} fusion(bf16[1024,394]{0,1:T(8,128)(2,1)S(1)} %copy-done, f32[4096,394]{0,1:T(8,128)} %get-tuple-element.13, f32[4096]{0:T(1024)S(1)} %broadcast_divide_fusion, f32[4096]{0:T(1024)S(1)} %get-tuple-element.11, s32[4096]{0:T(1024)S(1)} %all-reduce.1, f32[4096]{0:T(1024)S(1)} %pmax.7, s32[394]{0:T(512)S(1)} %iota_add_fusion), kind=kOutput, calls=%fused_computation.29 | convolution fusion | flops 3316408320 | bytes 24106536 | tf_op jit(solution)/shard_map/dot_general | solution.py:37
  239.9 0.0 reduce-scatter.2.cloned.1.call-update
  240.0 10.1 %fusion.16 = f32[1024,394]{0,1:T(8,128)} fusion(bf16[4096,1024]{1,0:T(8,128)(2,1)} %all-gather.2.cloned.1.call-done, f32[4096,394]{0,1:T(8,128)} %get-tuple-element.13, f32[4096]{0:T(1024)S(1)} %broadcast_divide_fusion, f32[4096]{0:T(1024)S(1)} %get-tuple-element.11, s32[4096]{0:T(1024)S(1)} %all-reduce.1, f32[4096]{0:T(1024)S(1)} %pmax.7, ...), kind=kOutput, calls=%fused_computation.28 | convolution fusion | flops 3316408320 | bytes 16524840 | tf_op jit(solution)/shard_map/dot_general | solution.py:36
  250.0 658.8 %reduce-scatter.2.cloned.1.call-done = f32[32,1024]{1,0:T(8,128)} async-done(((f32[4096,1024]{1,0:T(8,128)}), f32[32,1024]{1,0:T(8,128)}) %reduce-scatter.2.cloned.1.call-update) | async-done | bytes 131088 | tf_op jit(solution)/shard_map/reduce_scatter | solution.py:38
  908.8 1.1 fusion.14
  909.9 62.6 %all-reduce.2 = (f32[4096]{0:T(1024)S(1)}, f32[1024]{0:T(1024)}) all-reduce(f32[4096]{0:T(1024)S(1)} %get-tuple-element.5, f32[1024]{0:T(1024)S(1)} %get-tuple-element.6), channel_id=1, replica_groups=mesh['dp'=1,'vp'=128] {'vp'}, use_global_device_ids=true, to_apply=%region_7.8 | all-reduce | flops 5120 | bytes 40960 | tf_op jit(solution)/shard_map/psum | solution.py:30
  972.5 1.3 multiply_reduce_fusion
  973.8 1.6 fusion.13
  (11 shorter events, 0.0 us)
Async XLA Ops:
  7.2 76.9 %copy-start = (bf16[1024,394]{0,1:T(8,128)(2,1)S(1)}, bf16[1024,394]{0,1:T(8,128)(2,1)}, u32[]{:S(2)}) copy-start(bf16[1024,394]{0,1:T(8,128)(2,1)} %param.9) | copy-start | bytes 2420740
  7.2 76.9 %all-gather.2.cloned.1.call-start = ((), (), s32[]{:S(2)}) async-start(), calls=%async_computation.1 | async-start | bytes 8454144 | tf_op jit(solution)/shard_map/all_gather | solution.py:20
  9.8 898.9 %reduce-scatter.2.cloned.1.call-start = ((), (), s32[]{:S(2)}) async-start(), calls=%async_computation.2 | async-start | bytes 16908288 | tf_op jit(solution)/shard_map/reduce_scatter | solution.py:38
  239.9 668.8 %copy-start.1 = (bf16[32,1024]{1,0:T(8,128)(2,1)S(1)}, bf16[32,1024]{1,0:T(8,128)(2,1)}, u32[]{:S(2)}) copy-start(bf16[32,1024]{1,0:T(8,128)(2,1)} %param.5) | copy-start | bytes 196612
  239.9 668.8 %copy-start.2 = (f32[1024]{0:T(1024)S(1)}, f32[1024]{0:T(1024)}, u32[]{:S(2)}) copy-start(f32[1024]{0:T(1024)} %param.8) | copy-start | bytes 12292
Sparse Core Ops, SparseCore 0:
  11.5 72.4 all-gather.1
  240.1 668.6 reduce-scatter.1
where the time goes:
time: 983 us; the launch traced here: 982 us
  waiting for transfers between devices  662 us (67%)
  blocking collectives  259 us (26%)
  matrix products  33.3 us (3%)
  between operations  14.1 us (1%)
  other arithmetic  11.6 us (1%)
    reduce_scatter x1, waiting for transfers between devices, local_step(): d_normed = lax.psum_scatter(d_part, 'vp', scatter_dimension=0, tiled=True)  659 us
    unnamed x2, blocking collectives  133 us
    pmax x1, blocking collectives, local_step(): row_max = lax.pmax(jnp.max(logits, axis=1), 'vp')  63.3 us
    psum x1, blocking collectives, local_step(): target = lax.psum(jnp.sum(jnp.where(is_target, logits, 0.0), axis=1), 'vp')  62.6 us
  transfers between devices with their start and end apart: 2, of which 2 were waited for; matrix products, arithmetic and copies ran while one was open for 1% of the time, Pallas kernels for 0%

commit v1 on v0

v1 whole, which is shorter than its diff:
```python
import functools

import jax
import jax.numpy as jnp
from jax import lax
from jax.experimental import pallas as pl
from jax.experimental.pallas import tpu as pltpu
from jax.sharding import PartitionSpec as P

NORM_EPS = 1e-5
PAD_COLS = 128
RING = 4
MESH = pl.DeviceIdType.MESH
F32 = jnp.float32
BF16 = jnp.bfloat16


def _parts(depth):
    tiles = depth // 128
    a = -(-tiles // 3)
    b = -(-(tiles - a) // 2)
    cuts = (0, a * 128, (a + b) * 128, depth)
    return tuple((cuts[i], cuts[i + 1] - cuts[i]) for i in range(3))


class _Sems:
    def __init__(self, send, recv):
        self.send, self.recv, self.used, self.open = send, recv, 0, []

    def copy(self, src, dst, device):
        k = self.used
        self.used += 1
        c = pltpu.make_async_remote_copy(
            src_ref=src, dst_ref=dst, send_sem=self.send.at[k], recv_sem=self.recv.at[k],
            device_id={"vp": device}, device_id_type=MESH)
        c.start()
        self.open.append(c)
        return c

    def drain(self):
        for c in self.open:
            c.wait_send()
        self.open = []


def _kernel(dims, hid_ref, meta_ref, gain_ref, w_ref,
            red_ref, dh_ref, dw_ref,
            acts, meta, w2, ex, dz, gp, dwp, dwrx, dwo, labc, wtc, frow, lrow,
            stat, statrx, ssum, redbuf, redrx, accbuf,
            rxa, rxb, rxc, rx2a, rx2b, rx2c, rx3,
            send_sem, recv_sem, out_sem):
    rows, depth, vloc, vpad = dims
    nblk = 512
    parts = _parts(depth)
    me = lax.axis_index("vp")
    core = lax.rem(me, 2)
    chip = me // 2
    pos = (lax.rem(chip, 4), lax.rem(chip // 4, 4), chip // 16)
    stride = (2, 8, 32)
    other = me + 1 - 2 * core

    def peer(d, step):
        q = lax.rem(pos[d] + step + 4, 4)
        return me + (q - pos[d]) * stride[d]

    def at(d, step):
        return lax.rem(pos[d] + step + 4, 4)

    def sel(**kw):
        full = {0: slice(None), 1: slice(None), 2: slice(None)}
        for k, v in kw.items():
            full[int(k[1])] = v
        return (full[2], full[1], full[0])

    def pick(pairs):
        full = {0: slice(None), 1: slice(None), 2: slice(None)}
        full.update(dict(pairs))
        return (full[2], full[1], full[0])

    sems = _Sems(send_sem, recv_sem)

    barrier = pltpu.get_barrier_semaphore()
    peers = [peer(d, s) for d in range(3) for s in (1, 2, 3)] + [other]
    for p in peers:
        pl.semaphore_signal(barrier, inc=1, device_id={"vp": p}, device_id_type=MESH)

    x = hid_ref[...].astype(F32)
    gain = gain_ref[...]
    inv = lax.rsqrt(jnp.mean(x * x, axis=-1, keepdims=True) + NORM_EPS)
    acts[pos[2], pos[1], pos[0]] = (x * inv * gain).astype(BF16)
    meta[pos[2], pos[1], pos[0]] = meta_ref[...]
    w2[core, 0:vloc, :] = w_ref[...]
    w2[core, vloc:, :] = jnp.zeros((nblk - vloc, depth), BF16)
    pl.semaphore_wait(barrier, len(peers))

    def asl(pairs, c):
        return acts.at[(*pick(pairs), slice(None), pl.ds(*c))]

    h0, h1 = slice(0, 2), slice(2, 4)
    first = []
    for r, c in enumerate(parts):
        d0 = r
        own = {0: pos[0], 1: pos[1], 2: pos[2]}
        cs = []
        for s in (1, 3, 2):
            cs.append(sems.copy(asl(own, c), asl(own, c), peer(d0, s)))
        if r == 0:
            m = meta.at[pick(own)]
            for s in (1, 3, 2):
                cs.append(sems.copy(m, m, peer(d0, s)))
        first.append(cs)
    wcopy = sems.copy(w2.at[core], w2.at[core], other)

    def ag_ring(view, d, base, hd, kind):
        src = view({**base, d: pos[d]})
        return [sems.copy(src, src, peer(d, 1)), sems.copy(src, src, peer(d, 3))]

    def ag_forward(view, d, base, hd, cs):
        cs[0].wait_recv()
        v = view({**base, d: at(d, 3), hd: h0})
        cs.append(sems.copy(v, v, peer(d, 1)))
        cs[1].wait_recv()
        v = view({**base, d: at(d, 1), hd: h1})
        cs.append(sems.copy(v, v, peer(d, 3)))

    def ag_finish(cs):
        cs[2].wait_recv()
        cs[3].wait_recv()

    def mview(pairs):
        return meta.at[pick(pairs)]

    for phase in (1, 2):
        live = []
        for r, c in enumerate(parts):
            d0, d1, d2 = r, (r + 1) % 3, (r + 2) % 3
            d = d1 if phase == 1 else d2
            base = {d2: pos[d2]} if phase == 1 else {}
            views = [functools.partial(asl, c=c)] + ([mview] if r == 0 else [])
            if phase == 1:
                for cp in first[r]:
                    cp.wait_recv()
            else:
                for item in prev[r]:
                    ag_finish(item[4])
            live.append([[v, d, base, d0, ag_ring(v, d, base, d0, None)] for v in views])
        for r in range(3):
            for v, d, base, d0, cs in live[r]:
                ag_forward(v, d, base, d0, cs)
        prev = live
    for r in range(3):
        for item in prev[r]:
            ag_finish(item[4])
    wcopy.wait_recv()

    lane = lax.broadcasted_iota(jnp.int32, (rows, 128), 1)
    row = lax.broadcasted_iota(jnp.int32, (rows, 128), 0)

    mall = meta[...].reshape(64, 128)
    lane64 = lax.broadcasted_iota(jnp.int32, (64, 128), 1)
    part_sum = jnp.sum(jnp.where((lane64 >= rows) & (lane64 < 2 * rows), mall, 0.0), axis=0, keepdims=True)
    ssum[0] = part_sum
    scopy = sems.copy(ssum.at[0], ssum.at[1], other)

    def zdot(z, _):
        a = acts[z].reshape(16 * rows, depth)
        for b in range(2):
            ex[b, z] = lax.dot_general(a, w2[b], (((1,), (1,)), ((), ())),
                                       preferred_element_type=F32).reshape(4, 4, rows, nblk)
        return 0

    lax.fori_loop(0, 4, zdot, 0)

    lane_n = lax.broadcasted_iota(jnp.int32, (rows, nblk), 1)
    bases = [(2 * chip + b) * vloc for b in range(2)]
    accbuf[...] = jnp.zeros_like(accbuf)

    def soft(i, _):
        z, y = i // 4, lax.rem(i, 4)
        mrow = jnp.zeros((1, 128), F32)
        srow = jnp.zeros((1, 128), F32)
        for xx in range(4):
            mt = jnp.broadcast_to(meta[z, y, xx], (rows, 128))
            lab = jnp.sum(jnp.where(lane == row, mt, 0.0), axis=1, keepdims=True)
            wt = jnp.sum(jnp.where(lane == row + rows, mt, 0.0), axis=1, keepdims=True)
            labc[z, y, xx] = lab
            wtc[z, y, xx] = wt
            labi = lab.astype(jnp.int32)
            vals = []
            tgt = jnp.zeros((rows, nblk), F32)
            for b in range(2):
                v = ex[b, z, y, xx]
                ok = (lane_n < vloc) & (lane_n < vpad - bases[b])
                tgt = tgt + jnp.where((lane_n == labi - bases[b]) & (lane_n < vloc), v, 0.0)
                vals.append(jnp.where(ok, v, -jnp.inf))
            mx = jnp.max(jnp.maximum(vals[0], vals[1]), axis=1, keepdims=True)
            es = [jnp.exp(v - mx) for v in vals]
            sm = jnp.sum(es[0] + es[1], axis=1, keepdims=True)
            for b in range(2):
                ex[b, z, y, xx] = es[b]
            here = lane == row + rows * xx
            mrow = mrow + jnp.sum(jnp.where(here, mx, 0.0), axis=0, keepdims=True)
            srow = srow + jnp.sum(jnp.where(here, sm, 0.0), axis=0, keepdims=True)
            accbuf[0] += tgt * wt
        stat[0, 0, z, y] = mrow
        stat[0, 1, z, y] = srow
        return 0

    lax.fori_loop(0, 16, soft, 0)

    for d in range(3):
        cs = [sems.copy(stat.at[d], statrx.at[d, s - 1], peer(d, s)) for s in (1, 2, 3)]
        ms, ss = [stat[d, 0]], [stat[d, 1]]
        for s in range(3):
            cs[s].wait_recv()
            ms.append(statrx[d, s, 0])
            ss.append(statrx[d, s, 1])
        top = functools.reduce(jnp.maximum, ms)
        tot = functools.reduce(jnp.add, [s * jnp.exp(m - top) for m, s in zip(ms, ss)])
        stat[d + 1, 0] = top
        stat[d + 1, 1] = tot
    lse = stat[3, 0] + jnp.log(stat[3, 1])
    lrow[...] = lse
    frow[...] = jnp.exp(stat[0, 0] - lse)
    scopy.wait_recv()
    total_w = jnp.sum(ssum[0] + ssum[1], axis=1, keepdims=True)

    def grad(i, _):
        z, y = i // 4, lax.rem(i, 4)
        fr = jnp.broadcast_to(frow[z, y], (rows, 128))
        lr = jnp.broadcast_to(lrow[z, y], (rows, 128))
        for xx in range(4):
            here = lane == row + rows * xx
            fc = jnp.sum(jnp.where(here, fr, 0.0), axis=1, keepdims=True)
            lab = labc[z, y, xx].astype(jnp.int32)
            sc = wtc[z, y, xx] / total_w
            accbuf[1, :, 0:128] += jnp.where(here, lr, 0.0) * sc
            for b in range(2):
                p = ex[b, z, y, xx] * fc
                hit = (lane_n == lab - bases[b]) & (lane_n < vloc)
                dz[b, z, y, xx] = ((p - jnp.where(hit, 1.0, 0.0)) * sc).astype(BF16)
        return 0

    lax.fori_loop(0, 16, grad, 0)

    def gdot(z, _):
        g = jnp.dot(dz[0, z].reshape(16 * rows, nblk), w2[0], preferred_element_type=F32)
        g = g + jnp.dot(dz[1, z].reshape(16 * rows, nblk), w2[1], preferred_element_type=F32)
        gp[z] = g.reshape(4, 4, rows, depth)
        return 0

    lax.fori_loop(0, 4, gdot, 0)

    rx1s = (rxa, rxb, rxc)
    rx2s = (rx2a, rx2b, rx2c)

    def gsl(pairs, c):
        return gp.at[(*pick(pairs), slice(None), pl.ds(*c))]

    def rs_start(bufs, c, d, hd, base):
        far = at(d, 2)
        up, dn = at(d, 1), at(d, 3)
        return [
            sems.copy(gsl({**base, d: far, hd: h0}, c), bufs.at[0], peer(d, 1)),
            sems.copy(gsl({**base, d: far, hd: h1}, c), bufs.at[1], peer(d, 3)),
            sems.copy(gsl({**base, d: up, hd: h1}, c), bufs.at[2], peer(d, 1)),
            sems.copy(gsl({**base, d: dn, hd: h0}, c), bufs.at[3], peer(d, 3)),
        ]

    def each(hd, rest, half, fixed, fn):
        if rest is None:
            for i in range(2):
                fn((i,), {**fixed, hd: 2 * half + i})
            return

        def body(t, _):
            i, j = t // 4, lax.rem(t, 4)
            idx = (i, j) if hd > rest else (j, i)
            fn(idx, {**fixed, hd: 2 * half + i, rest: j})
            return 0

        lax.fori_loop(0, 8, body, 0)

    def rs_relay(bufs, c, d, hd, rest, base, cs):
        for k, (q, half) in enumerate(((at(d, 1), 0), (at(d, 3), 1))):
            cs[k].wait_recv()

            def add(idx, pairs):
                bufs[(k, *idx)] += gp[(*pick(pairs), slice(None), pl.ds(*c))]

            each(hd, rest, half, {**base, d: q}, add)
            cs.append(sems.copy(bufs.at[k], bufs.at[4 + k], peer(d, 1 if k == 0 else 3)))

    def rs_finish(bufs, c, d, hd, rest, base, cs):
        for half, (k1, k2) in enumerate(((3, 4), (2, 5))):
            cs[k1].wait_recv()
            cs[k2].wait_recv()

            def add(idx, pairs):
                s = (*pick(pairs), slice(None), pl.ds(*c))
                gp[s] = gp[s] + (bufs[(k1, *idx)] + bufs[(k2, *idx)])

            each(hd, rest, half, {**base, d: pos[d]}, add)

    def order(r):
        return r, (r + 1) % 3, (r + 2) % 3

    cs1 = [rs_start(rx1s[r], c, order(r)[0], order(r)[1], {}) for r, c in enumerate(parts)]

    def dwdot(blk):
        dwp[blk] = jnp.zeros_like(dwp[blk])

        def body(z, _):
            dwp[blk] += lax.dot_general(dz[blk, z].reshape(16 * rows, nblk), acts[z].reshape(16 * rows, depth),
                                        (((0,), (0,)), ((), ())), preferred_element_type=F32)
            return 0

        lax.fori_loop(0, 4, body, 0)

    dwdot(1 - core)
    dwcopy = sems.copy(dwp.at[1 - core], dwrx, other)

    for r, c in enumerate(parts):
        d0, d1, d2 = order(r)
        rs_relay(rx1s[r], c, d0, d1, d2, {}, cs1[r])

    dwdot(core)
    dwcopy.wait_recv()
    dwo[...] = dwp[core, 0:vloc, :] + dwrx[0:vloc, :]
    ocopy = pltpu.make_async_copy(dwo, dw_ref, out_sem)
    ocopy.start()

    cs2 = []
    for r, c in enumerate(parts):
        d0, d1, d2 = order(r)
        rs_finish(rx1s[r], c, d0, d1, d2, {}, cs1[r])
        cs2.append(rs_start(rx2s[r], c, d1, d2, {d0: pos[d0]}))
    for r, c in enumerate(parts):
        d0, d1, d2 = order(r)
        rs_relay(rx2s[r], c, d1, d2, None, {d0: pos[d0]}, cs2[r])
    cs3 = []
    for r, c in enumerate(parts):
        d0, d1, d2 = order(r)
        base = {d0: pos[d0]}
        rs_finish(rx2s[r], c, d1, d2, None, base, cs2[r])
        base = {d0: pos[d0], d1: pos[d1]}
        cs3.append([sems.copy(gsl({**base, d2: at(d2, s)}, c), rx3.at[s - 1, :, pl.ds(*c)], peer(d2, s))
                    for s in (1, 3, 2)])
    for r in range(3):
        for cp in cs3[r]:
            cp.wait_recv()
    g = gp[pos[2], pos[1], pos[0]] + (rx3[0] + rx3[2]) + rx3[1]

    n = x * inv
    u = g * gain
    dh_ref[...] = (inv * (u - n * jnp.mean(u * n, axis=-1, keepdims=True))).astype(BF16)
    redbuf[0, 0:1, :] = jnp.sum(g * n, axis=0, keepdims=True)
    lsum = jnp.sum(accbuf[1]) * (1.0 / 64.0) - jnp.sum(accbuf[0] / total_w)
    redbuf[0, 1:2, :] = jnp.broadcast_to(lsum.reshape(1, 1), (1, depth))

    cp = sems.copy(redbuf.at[0], redrx.at[0], other)
    cp.wait_recv()
    redbuf[1] = redbuf[0] + redrx[0]
    for d in range(3):
        cs = [sems.copy(redbuf.at[1 + d], redrx.at[1 + 3 * d + s - 1], peer(d, s)) for s in (1, 2, 3)]
        for cp in cs:
            cp.wait_recv()
        tot = (redbuf[1 + d] + redrx[1 + 3 * d + 1]) + (redrx[1 + 3 * d] + redrx[1 + 3 * d + 2])
        if d < 2:
            redbuf[2 + d] = tot
        else:
            red_ref[...] = tot
    ocopy.wait()
    sems.drain()


def solution(mesh):
    def local_step(hidden, labels, loss_weight, norm_gain, w_local):
        rows, depth = hidden.shape
        vloc = w_local.shape[1]
        vpad = vloc * mesh.shape["vp"] - PAD_COLS
        meta = jnp.concatenate([labels.astype(F32), loss_weight, jnp.zeros((128 - 2 * rows,), F32)]).reshape(1, 128)
        nb = 512
        widths = [w for _, w in _parts(depth)]
        dma = pltpu.SemaphoreType.DMA
        nsem = 116
        v = pltpu.VMEM
        vm = pl.BlockSpec(memory_space=pltpu.VMEM)
        red, dh, dwt = pl.pallas_call(
            functools.partial(_kernel, (rows, depth, vloc, vpad)),
            name="head_step",
            out_shape=(jax.ShapeDtypeStruct((2, depth), F32),
                       jax.ShapeDtypeStruct((rows, depth), BF16),
                       jax.ShapeDtypeStruct((vloc, depth), F32)),
            in_specs=[vm] * 4,
            out_specs=(vm, vm, pl.BlockSpec(memory_space=pl.ANY)),
            scratch_shapes=[
                v((4, 4, 4, rows, depth), BF16),
                v((4, 4, 4, 1, 128), F32),
                v((2, nb, depth), BF16),
                v((2, 4, 4, 4, rows, nb), F32),
                v((2, 4, 4, 4, rows, nb), BF16),
                v((4, 4, 4, rows, depth), F32),
                v((2, nb, depth), F32),
                v((nb, depth), F32),
                v((vloc, depth), F32),
                v((4, 4, 4, rows, 1), F32),
                v((4, 4, 4, rows, 1), F32),
                v((4, 4, 1, 128), F32),
                v((4, 4, 1, 128), F32),
                v((4, 2, 4, 4, 1, 128), F32),
                v((3, 3, 2, 4, 4, 1, 128), F32),
                v((2, 1, 128), F32),
                v((4, 2, depth), F32),
                v((10, 2, depth), F32),
                v((2, rows, nb), F32),
                v((6, 4, 2, rows, widths[0]), F32),
                v((6, 2, 4, rows, widths[1]), F32),
                v((6, 4, 2, rows, widths[2]), F32),
                v((6, 2, rows, widths[0]), F32),
                v((6, 2, rows, widths[1]), F32),
                v((6, 2, rows, widths[2]), F32),
                v((3, rows, depth), F32),
                dma((nsem,)),
                dma((nsem,)),
                dma(()),
            ],
            compiler_params=pltpu.CompilerParams(
                collective_id=0, has_side_effects=True, vmem_limit_bytes=63 * 1024 * 1024),
        )(hidden, meta, norm_gain.reshape(1, depth), w_local.T)
        return red[1, 0:1], dh, dwt.T, red[0]

    return jax.shard_map(
        local_step,
        mesh=mesh,
        in_specs=(P(("dp", "vp"), None), P(("dp", "vp")), P(("dp", "vp")), P(None), P(None, "vp")),
        out_specs=(P("dp"), P(("dp", "vp"), None), P("dp", "vp"), P("dp")),
        check_vma=False,
    )
```

time: 983 us -> 123 us (0.13)
  waiting for transfers between devices: 662 us -> 0 us
  blocking collectives: 259 us -> 0 us
  Pallas kernels: 0 us -> 114 us
  matrix products: 33.3 us -> 0 us
  between operations: 14.1 us -> 0.64 us
    reduce_scatter x1 -> x0, waiting for transfers between devices: 659 us -> none  [local_step(): d_normed = lax.psum_scatter(d_part, 'vp', scatter_dimension=0, tiled=True)]
    unnamed x2 -> x0, blocking collectives: 133 us -> none
    pallas_call x0 -> x1, Pallas kernels: none -> 114 us  [local_step(): pl.pallas_call(functools.partial(_kernel, (rows, depth, vloc, vpad)), nam...]
    pmax x1 -> x0, blocking collectives: 63.3 us -> none  [local_step(): row_max = lax.pmax(jnp.max(logits, axis=1), 'vp')]
    psum x1 -> x0, blocking collectives: 62.6 us -> none  [local_step(): target = lax.psum(jnp.sum(jnp.where(is_target, logits, 0.0), axis=1), 'vp')]
    dot_general x3 -> x0, matrix products: 33.3 us -> none  [the longest x1 12.5 us: local_step(): lax.dot_general(d_logits, w_local, (((1,), (1,)), ((), ())), preferred_el...]
  transfers between devices with their start and end apart: 2 -> 0, of which waited for: 2 -> 0; matrix products, arithmetic and copies ran while one was open for 1% -> 0% of each run, Pallas kernels for 0% -> 0%
where the time goes in v1:
time: 123 us
  Pallas kernels  114 us (93%)
  local copies, waits for them, and re-layouts  6.73 us (5%)
  other arithmetic  1.9 us (2%)
    pallas_call x1, Pallas kernels, local_step(): pl.pallas_call(functools.partial(_kernel, (rows, depth, vloc, vpad)), nam...  114 us
    unnamed x2, local copies, waits for them, and re-layouts  4.25 us
    slice x2, local copies, waits for them, and re-layouts, local_step(): return (red[1, 0:1], dh, dwt.T, red[0])  2.47 us

profile of v1, /device:TPU:0, one launch (start us, length us, event | category | flops | bytes accessed | tf_op | source)
XLA Modules:
  0.0 122.8 jit_solution(3333898656689560665)
XLA Ops:
  0.6 0.7 convert_element_type.3
  1.3 1.2 %maximum_bitcast_fusion.meta_ref = f32[1,128]{1,0:T(1,128)} fusion(f32[64]{0:T(128)S(1)} %broadcast_in_dim.3, f32[32]{0:T(128)} %param.7, f32[32]{0:T(128)S(1)} %convert_element_type.3), kind=kLoop, calls=%fused_computation | loop fusion | flops 256 | bytes 1024 | tf_op jit(solution)/shard_map/reshape | solution.py:382
  2.5 113.5 %head_step.1 = (f32[2,1024]{1,0:T(2,128)}, bf16[32,1024]{1,0:T(8,128)(2,1)}, f32[394,1024]{1,0:T(8,128)}) custom-call(bf16[32,1024]{1,0:T(8,128)(2,1)} %hid_ref.1, f32[1,128]{1,0:T(1,128)} %maximum_bitcast_fusion.meta_ref, f32[1,1024]{1,0:T(1,128)} %bitcast.9, bf16[394,1024]{1,0:T(8,128)(2,1)} %bitcast.8), custom_call_target="tpu_custom_call" | custom-call | tf_op jit(solution)/shard_map/head_step/pallas_call | solution.py:389
  116.1 1.3 %slice.7 = f32[1,1024]{1,0:T(1,128)} slice(f32[2,1024]{1,0:T(2,128)} %get-tuple-element.7), slice={[0:1], [0:1024]} | slice | bytes 8192 | tf_op jit(solution)/shard_map/slice | solution.py:431
  117.4 1.2 slice.6
  118.6 1.5 %copy.11 = bf16[32,1024]{1,0:T(8,128)(2,1)} copy(bf16[32,1024]{1,0:T(8,128)(2,1)} %get-tuple-element.15) | data formatting | bytes 131072
  120.0 2.8 %copy.12 = f32[1024,394]{0,1:T(8,128)} copy(f32[1024,394]{0,1:T(8,128)} %bitcast.7) | data formatting | bytes 3227648
  (1 shorter events, 0.0 us)

commit v2 on v0

v2 whole, which is shorter than its diff:
```python
import functools
import math

import jax
import jax.numpy as jnp
from jax import lax
from jax.experimental import pallas as pl
from jax.experimental.pallas import tpu as pltpu
from jax.sharding import PartitionSpec as P

NORM_EPS = 1e-5
PAD_COLS = 128
CHUNKS = 4
NBLK = 512
MESH = pl.DeviceIdType.MESH
F32 = jnp.float32
BF16 = jnp.bfloat16
AROUND = (1, 3, 2)


def _parts(depth, k):
    tiles = depth // 128
    sizes = [tiles // 3 + (1 if i < tiles % 3 else 0) for i in range(3)]
    sizes = [sizes[(i + k) % 3] for i in range(3)]
    starts = [0, sizes[0], sizes[0] + sizes[1]]
    return tuple((a * 128, n * 128) for a, n in zip(starts, sizes))


def _rowsum(x):
    return jnp.sum(x, axis=1, keepdims=True)


def _colsum(x):
    return jnp.sum(x, axis=0, keepdims=True)


def _scratch(rows, depth, vloc):
    r = rows // CHUNKS
    v = pltpu.VMEM
    c = CHUNKS
    s = {
        "xs": v((c, 4, 4, 4, r, depth), BF16),
        "acts": v((c, 4, 4, 4 * r, depth), BF16),
        "meta": v((4, 4, 4, 2, 128), F32),
        "win": v((vloc, depth), BF16),
        "w2": v((2, NBLK, depth), BF16),
        "ex": v((c, 2, 4, 4, 4, r, NBLK), F32),
        "dz": v((c, 2, 4, 4, 4 * r, NBLK), BF16),
        "gp": v((c, 4, 4, 4, r, depth), F32),
        "dwp": v((2, NBLK, depth), F32),
        "dwrx": v((NBLK, depth), F32),
        "dwo": v((vloc, depth), F32),
        "labc": v((c, 4, 4, 4 * r, 1), F32),
        "wtc": v((c, 4, 4, 4 * r, 1), F32),
        "rcol": v((c, 4, 4, 4 * r, 1), F32),
        "frow": v((c, 4, 1, 128), F32),
        "lrow": v((c, 4, 1, 128), F32),
        "stat": v((c, 4, 2, 4, 1, 128), F32),
        "statrx": v((c, 3, 3, 2, 4, 1, 128), F32),
        "ssum": v((2, 1, 128), F32),
        "dgacc": v((r, depth), F32),
        "redbuf": v((4, 2, depth), F32),
        "redrx": v((10, 2, depth), F32),
        "acct": v((4 * r, NBLK), F32),
        "accl": v((4 * r, 128), F32),
        "rx3": v((c, 3, r, depth), F32),
    }
    for k in range(c):
        for p, (_, w) in enumerate(_parts(depth, k)):
            shape = (2, 4) if p == 1 else (4, 2)
            s[f"rx1_{k}_{p}"] = v((6, *shape, r, w), F32)
            s[f"rx2_{k}_{p}"] = v((3, 4, r, w) if k == c - 1 else (6, 2, r, w), F32)
    n = 400
    s["send_sem"] = pltpu.SemaphoreType.DMA((n,))
    s["recv_sem"] = pltpu.SemaphoreType.DMA((n,))
    s["loc_sem"] = pltpu.SemaphoreType.DMA((2,))
    return s


def _pick(pairs):
    return tuple(pairs.get(d, slice(None)) for d in (2, 1, 0))


def _interleave(procs, hop=2.6, rate=46.0):
    now, link = 0.0, 0.0
    ready = [now] * len(procs)
    busy = [False] * len(procs)
    alive = set(range(len(procs)))
    while alive:
        able = [i for i in alive if ready[i] <= now]
        if able:
            i = min(able, key=lambda i: (busy[i], i))
        else:
            i = min(alive, key=lambda i: (ready[i], i))
            now = ready[i]
        try:
            step = next(procs[i])
        except StopIteration:
            alive.discard(i)
            continue
        if step is None:
            ready[i] = now + 1
            continue
        now += step[0]
        busy[i] = len(step) == 1
        ready[i] = now
        if not busy[i]:
            start = max(now, link)
            ready[i] = start + step[1] / rate + hop
            link = start + step[-1] / rate


def _kernel(dims, names, lab_ref, wt_ref, hid_ref, gain_ref, w_ref, red_ref, dh_ref, dw_ref, *refs):
    rows, depth, vloc, vreal = dims
    s = dict(zip(names, refs))
    r8 = rows // CHUNKS
    r32 = 4 * r8
    xs, acts, meta, w2, ex, dz, gp = (s[n] for n in ("xs", "acts", "meta", "w2", "ex", "dz", "gp"))
    dwp, stat, statrx, ssum = s["dwp"], s["stat"], s["statrx"], s["ssum"]
    me = lax.axis_index("vp")
    core = lax.rem(me, 2)
    chip = me // 2
    pos = (lax.rem(chip, 4), lax.rem(chip // 4, 4), chip // 16)
    stride = (2, 8, 32)
    other = me + 1 - 2 * core
    own = {0: pos[0], 1: pos[1], 2: pos[2]}
    h0, h1 = slice(0, 2), slice(2, 4)

    def at(d, step):
        return lax.rem(pos[d] + step, 4)

    def peer(d, step):
        return me + (at(d, step) - pos[d]) * stride[d]

    opened = []

    def copy(src, dst, device):
        i = len(opened)
        c = pltpu.make_async_remote_copy(
            src_ref=src, dst_ref=dst, send_sem=s["send_sem"].at[i], recv_sem=s["recv_sem"].at[i],
            device_id={"vp": device}, device_id_type=MESH)
        c.start()
        opened.append(c)
        return c

    barrier = pltpu.get_barrier_semaphore()
    peers = [peer(d, t) for d in range(3) for t in AROUND] + [other]
    for p in peers:
        pl.semaphore_signal(barrier, inc=1, device_id={"vp": p}, device_id_type=MESH)
    wload = pltpu.make_async_copy(w_ref, s["win"], s["loc_sem"].at[0])
    wload.start()

    for k in range(CHUNKS):
        xs[k, pos[2], pos[1], pos[0]] = hid_ref[k * r8:(k + 1) * r8, :]
    mine = meta.at[pos[2], pos[1], pos[0]]
    mine[...] = jnp.zeros((2, 128), F32)
    mine[0:1, 0:rows] = lab_ref[...].astype(F32)
    mine[1:2, 0:rows] = wt_ref[...]
    for n in ("dgacc", "acct", "accl"):
        s[n][...] = jnp.zeros_like(s[n])
    gain = gain_ref[...]
    pl.semaphore_wait(barrier, len(peers))

    lane = lax.broadcasted_iota(jnp.int32, (r32, 128), 1)
    row = lax.broadcasted_iota(jnp.int32, (r32, 128), 0)
    lane_n = lax.broadcasted_iota(jnp.int32, (r32, NBLK), 1)
    bases = [(2 * chip + b) * vloc for b in range(2)]
    done = {"g": 0, "dz": 0}
    shared = {}

    def mview(pairs):
        return meta.at[_pick(pairs)]

    def order(p):
        return p, (p + 1) % 3, (p + 2) % 3

    def half_mat(fn):
        lax.fori_loop(0, 2, lambda i, _: (fn(i), 0)[1], 0)

    def w_proc():
        yield 0.1,
        wload.wait()
        w2[core, 0:vloc, :] = s["win"][...]
        w2[core, vloc:, :] = jnp.zeros((NBLK - vloc, depth), BF16)
        shared["w"] = copy(w2.at[core], w2.at[core], other)
        yield 0.3,

    def chunk(k):
        parts = _parts(depth, k)
        wide = max(w for _, w in parts)
        kb = r8 * wide * 2 / 1024
        last = k == CHUNKS - 1

        def xsl(c, pairs):
            return xs.at[(k, *_pick(pairs), slice(None), pl.ds(*c))]

        def spread(view, pairs, d, src=None):
            ref = view(pairs) if src is None else src
            return [copy(ref, view(pairs), peer(d, t)) for t in AROUND]

        def views(p):
            return [functools.partial(xsl, parts[p])] + [mview] * (p + k == 0)

        def settle():
            for cp in flight:
                cp.wait_recv()
            flight.clear()

        flight = []
        for p, c in enumerate(parts):
            flight += spread(views(p)[0], own, p, hid_ref.at[pl.ds(k * r8, r8), pl.ds(*c)])
            for vw in views(p)[1:]:
                flight += spread(vw, own, p)
        yield 0.1, 2 * kb
        settle()
        for p in range(3):
            _, d, d2 = order(p)
            for vw in views(p):
                flight += spread(vw, {d: pos[d], d2: pos[d2]}, d)
        yield 0.1, 8 * kb
        settle()
        ring = []
        for p in range(3):
            d0, _, d = order(p)
            for vw in views(p):
                if k == 0:
                    flight += spread(vw, {d: pos[d]}, d)
                else:
                    src = vw({d: pos[d]})
                    ring.append((vw, d, d0, [copy(src, src, peer(d, t)) for t in (1, 3)]))
        yield (0.1, 32 * kb) if k == 0 else (0.1, 16 * kb)
        for vw, d, d0, cs in ring:
            for i, (t, h) in enumerate(((1, h0), (3, h1))):
                cs[i].wait_recv()
                vv = vw({d: at(d, 4 - t), d0: h})
                flight.append(copy(vv, vv, peer(d, t)))
        if k:
            yield 0.1, 8 * kb
        settle()

        def norm(i, _):
            z, y = i // 4, lax.rem(i, 4)
            x = xs[k, z, y].astype(F32).reshape(r32, depth)
            inv = lax.rsqrt(jnp.mean(x * x, axis=-1, keepdims=True) + NORM_EPS)
            s["rcol"][k, z, y] = inv
            acts[k, z, y] = (x * inv * gain).astype(BF16)
            return 0

        lax.fori_loop(0, 16, norm, 0)
        if k == 0:
            mall = meta[...].reshape(128, 128)
            odd = lax.rem(lax.broadcasted_iota(jnp.int32, (128, 128), 0), 2) == 1
            ssum[0] = _colsum(jnp.where(odd, mall, 0.0))
            shared["s"] = copy(ssum.at[0], ssum.at[1], other)
            shared["w"].wait_recv()
        yield 0.7,

        def zdot(i):
            a = acts[k, pl.ds(2 * i, 2)].reshape(8 * r32, depth)
            for b in range(2):
                ex[k, b, pl.ds(2 * i, 2)] = lax.dot_general(
                    a, w2[b], (((1,), (1,)), ((), ())),
                    preferred_element_type=F32).reshape(2, 4, 4, r8, NBLK)

        half_mat(zdot)
        yield 1.4,

        def soft(z, _):
            mrow = jnp.zeros((1, 128), F32)
            srow = jnp.zeros((1, 128), F32)
            for y in range(4):
                def col(j):
                    m = jnp.broadcast_to(meta[z, y, :, j:j + 1, :], (4, r8, 128)).reshape(r32, 128)
                    return _rowsum(jnp.where(lane == k * r8 + lax.rem(row, r8), m, 0.0))

                lab, wt = col(0), col(1)
                s["labc"][k, z, y] = lab
                s["wtc"][k, z, y] = wt
                labi = lab.astype(jnp.int32)
                vals = []
                tgt = jnp.zeros((r32, NBLK), F32)
                for b in range(2):
                    val = ex[k, b, z, y].reshape(r32, NBLK)
                    ok = (lane_n < vloc) & (lane_n < vreal - bases[b])
                    tgt = tgt + jnp.where((lane_n == labi - bases[b]) & (lane_n < vloc), val, 0.0)
                    vals.append(jnp.where(ok, val, -jnp.inf))
                mx = jnp.max(jnp.maximum(vals[0], vals[1]), axis=1, keepdims=True)
                es = [jnp.exp(val - mx) for val in vals]
                sm = _rowsum(es[0] + es[1])
                for b in range(2):
                    ex[k, b, z, y] = es[b].reshape(4, r8, NBLK)
                here = lane == row + r32 * y
                mrow = mrow + _colsum(jnp.where(here, mx, 0.0))
                srow = srow + _colsum(jnp.where(here, sm, 0.0))
                s["acct"][...] += tgt * wt
            stat[k, 0, 0, z] = mrow
            stat[k, 0, 1, z] = srow
            return 0

        lax.fori_loop(0, 4, soft, 0)
        cost = 1.2
        for d in range(3):
            cs = [copy(stat.at[k, d], statrx.at[k, d, i], peer(d, t)) for i, t in enumerate(AROUND)]
            yield cost, 8
            ms, ss = [stat[k, d, 0]], [stat[k, d, 1]]
            for i, cp in enumerate(cs):
                cp.wait_recv()
                ms.append(statrx[k, d, i, 0])
                ss.append(statrx[k, d, i, 1])
            top = functools.reduce(jnp.maximum, ms)
            stat[k, d + 1, 0] = top
            stat[k, d + 1, 1] = functools.reduce(jnp.add, [b * jnp.exp(a - top) for a, b in zip(ms, ss)])
            cost = 0.2
        lse = stat[k, 3, 0] + jnp.log(stat[k, 3, 1])
        s["lrow"][k] = lse
        s["frow"][k] = jnp.exp(stat[k, 0, 0] - lse)
        if k == 0:
            shared["s"].wait_recv()
        total_w = _rowsum(ssum[0] + ssum[1])

        def grad(z, _):
            for y in range(4):
                here = lane == row + r32 * y
                fr = jnp.broadcast_to(s["frow"][k, z], (r32, 128))
                lr = jnp.broadcast_to(s["lrow"][k, z], (r32, 128))
                fc = _rowsum(jnp.where(here, fr, 0.0))
                lab = s["labc"][k, z, y].astype(jnp.int32)
                sc = s["wtc"][k, z, y] / total_w
                s["accl"][...] += jnp.where(here, lr, 0.0) * sc
                for b in range(2):
                    prob = ex[k, b, z, y].reshape(r32, NBLK) * fc
                    hit = (lane_n == lab - bases[b]) & (lane_n < vloc)
                    dz[k, b, z, y] = ((prob - jnp.where(hit, 1.0, 0.0)) * sc).astype(BF16)
            return 0

        lax.fori_loop(0, 4, grad, 0)
        done["dz"] += 1

        def gdot(i):
            zz = pl.ds(2 * i, 2)
            g = jnp.dot(dz[k, 0, zz].reshape(8 * r32, NBLK), w2[0], preferred_element_type=F32)
            g = g + jnp.dot(dz[k, 1, zz].reshape(8 * r32, NBLK), w2[1], preferred_element_type=F32)
            gp[k, zz] = g.reshape(2, 4, 4, r8, depth)

        half_mat(gdot)

        def gsl(c, pairs):
            return gp.at[(k, *_pick(pairs), slice(None), pl.ds(*c))]

        def rs_start(bufs, c, d, hd, base):
            far, up, dn = at(d, 2), at(d, 1), at(d, 3)
            return [
                copy(gsl(c, {**base, d: far, hd: h0}), bufs.at[0], peer(d, 1)),
                copy(gsl(c, {**base, d: far, hd: h1}), bufs.at[1], peer(d, 3)),
                copy(gsl(c, {**base, d: up, hd: h1}), bufs.at[2], peer(d, 1)),
                copy(gsl(c, {**base, d: dn, hd: h0}), bufs.at[3], peer(d, 3)),
            ]

        def each(hd, rest, half, fixed, fn):
            if rest is None:
                for i in range(2):
                    fn((i,), {**fixed, hd: 2 * half + i})
                return

            def body(t, _):
                i, j = t // 4, lax.rem(t, 4)
                fn((i, j) if hd > rest else (j, i), {**fixed, hd: 2 * half + i, rest: j})
                return 0

            lax.fori_loop(0, 8, body, 0)

        def rs_relay(bufs, c, d, hd, rest, base, cs):
            for i, (q, half) in enumerate(((at(d, 1), 0), (at(d, 3), 1))):
                cs[i].wait_recv()

                def add(idx, pairs):
                    bufs[(i, *idx)] += gp[(k, *_pick(pairs), slice(None), pl.ds(*c))]

                each(hd, rest, half, {**base, d: q}, add)
                cs.append(copy(bufs.at[i], bufs.at[4 + i], peer(d, 1 if i == 0 else 3)))

        def rs_finish(bufs, c, d, hd, rest, base, cs):
            for half, (k1, k2) in enumerate(((3, 4), (2, 5))):
                cs[k1].wait_recv()
                cs[k2].wait_recv()

                def add(idx, pairs):
                    sl = (k, *_pick(pairs), slice(None), pl.ds(*c))
                    gp[sl] = gp[sl] + (bufs[(k1, *idx)] + bufs[(k2, *idx)])

                each(hd, rest, half, {**base, d: pos[d]}, add)

        rx1 = [s[f"rx1_{k}_{p}"] for p in range(3)]
        rx2 = [s[f"rx2_{k}_{p}"] for p in range(3)]
        cs1 = [rs_start(rx1[p], c, order(p)[0], order(p)[1], {}) for p, c in enumerate(parts)]
        yield 2.2, 16 * kb, 32 * kb

        def dg(i, _):
            z, y = i // 4, lax.rem(i, 4)
            n = xs[k, z, y].astype(F32).reshape(r32, depth) * s["rcol"][k, z, y]
            t = gp[k, z, y].reshape(r32, depth) * n
            s["dgacc"][...] += jnp.sum(t.reshape(4, r8, depth), axis=0)
            return 0

        lax.fori_loop(0, 16, dg, 0)
        done["g"] += 1
        for p, c in enumerate(parts):
            d0, d1, d2 = order(p)
            rs_relay(rx1[p], c, d0, d1, d2, {}, cs1[p])
        yield 0.7, 16 * kb
        cs2 = []
        for p, c in enumerate(parts):
            d0, d1, d2 = order(p)
            rs_finish(rx1[p], c, d0, d1, d2, {}, cs1[p])
            base = {d0: pos[d0]}
            if last:
                cs2.append([copy(gsl(c, {**base, d1: at(d1, t)}), rx2[p].at[i], peer(d1, t))
                            for i, t in enumerate(AROUND)])
            else:
                cs2.append(rs_start(rx2[p], c, d1, d2, base))
        yield (0.4, 16 * kb) if last else (0.4, 4 * kb, 8 * kb)
        if not last:
            for p, c in enumerate(parts):
                d0, d1, d2 = order(p)
                rs_relay(rx2[p], c, d1, d2, None, {d0: pos[d0]}, cs2[p])
            yield 0.2, 4 * kb
        cs3 = []
        for p, c in enumerate(parts):
            d0, d1, d2 = order(p)
            base = {d0: pos[d0], d1: pos[d1]}
            if last:
                for cp in cs2[p]:
                    cp.wait_recv()
                for j in range(4):
                    sl = (k, *_pick({**base, d2: j}), slice(None), pl.ds(*c))
                    gp[sl] = (gp[sl] + rx2[p][2, j]) + (rx2[p][0, j] + rx2[p][1, j])
            else:
                rs_finish(rx2[p], c, d1, d2, None, {d0: pos[d0]}, cs2[p])
            cs3 += [copy(gsl(c, {**base, d2: at(d2, t)}), s["rx3"].at[k, i, :, pl.ds(*c)], peer(d2, t))
                    for i, t in enumerate(AROUND)]
        yield 0.2, 4 * kb
        for cp in cs3:
            cp.wait_recv()
        g = gp[k, pos[2], pos[1], pos[0]] + (s["rx3"][k, 0] + s["rx3"][k, 1]) + s["rx3"][k, 2]
        x = hid_ref[k * r8:(k + 1) * r8, :].astype(F32)
        inv = lax.rsqrt(jnp.mean(x * x, axis=-1, keepdims=True) + NORM_EPS)
        n = x * inv
        u = g * gain
        dh_ref[k * r8:(k + 1) * r8, :] = (inv * (u - n * jnp.mean(u * n, axis=-1, keepdims=True))).astype(BF16)
        yield 0.3,

    def dw_proc():
        while done["dz"] < CHUNKS:
            yield None
        for first in (True, False):
            blk = 1 - core if first else core
            for k in range(CHUNKS):
                def part():
                    return lax.dot_general(dz[k, blk].reshape(16 * r32, NBLK), acts[k].reshape(16 * r32, depth),
                                           (((0,), (0,)), ((), ())), preferred_element_type=F32)

                if k == 0:
                    dwp[blk] = part()
                else:
                    dwp[blk] += part()
                if k < CHUNKS - 1:
                    yield 0.8,
            if first:
                cp = copy(dwp.at[blk], s["dwrx"], other)
            yield 0.8,
        cp.wait_recv()
        s["dwo"][...] = dwp[core, 0:vloc, :] + s["dwrx"][0:vloc, :]
        shared["o"] = pltpu.make_async_copy(s["dwo"], dw_ref, s["loc_sem"].at[1])
        shared["o"].start()
        yield 0.5,

    def red_proc():
        while done["g"] < CHUNKS:
            yield None
        redbuf, redrx = s["redbuf"], s["redrx"]
        total_w = _rowsum(ssum[0] + ssum[1])
        redbuf[0, 0:1, :] = _colsum(s["dgacc"][...])
        lsum = jnp.sum(s["accl"][...]) * (1.0 / 64.0) - jnp.sum(s["acct"][...] / total_w)
        redbuf[0, 1:2, :] = jnp.broadcast_to(lsum.reshape(1, 1), (1, depth))
        cp = copy(redbuf.at[0], redrx.at[0], other)
        yield 0.3, 1
        cp.wait_recv()
        redbuf[1] = redbuf[0] + redrx[0]
        for d in range(3):
            cs = [copy(redbuf.at[1 + d], redrx.at[1 + 3 * d + i], peer(d, t)) for i, t in enumerate(AROUND)]
            yield 0.1, 24
            for cp in cs:
                cp.wait_recv()
            tot = redbuf[1 + d] + jnp.sum(redrx[pl.ds(1 + 3 * d, 3)], axis=0)
            if d < 2:
                redbuf[2 + d] = tot
            else:
                red_ref[...] = tot

    _interleave([chunk(k) for k in range(CHUNKS)] + [w_proc(), red_proc(), dw_proc()])
    shared["o"].wait()
    for c in opened:
        c.wait_send()


def _finish(red_ref, dh_ref, dw_ref, loss_out, dh_out, dw_out, dg_out, buf, sem):
    get = pltpu.make_async_copy(dw_ref, buf, sem.at[0])
    get.start()
    loss_out[...] = red_ref[1:2, 0:1]
    dg_out[...] = red_ref[0:1, :]
    dh_out[...] = dh_ref[...]
    get.wait()
    put = pltpu.make_async_copy(buf, dw_out, sem.at[1])
    put.start()
    put.wait()


def solution(mesh):
    def local_step(hidden, labels, loss_weight, norm_gain, w_local):
        rows, depth = hidden.shape
        vloc = w_local.shape[1]
        vreal = vloc * mesh.shape["vp"] - PAD_COLS
        vm = pl.BlockSpec(memory_space=pltpu.VMEM)
        hbm = pl.BlockSpec(memory_space=pl.ANY)
        scratch = _scratch(rows, depth, vloc)
        red, dh, dwt = pl.pallas_call(
            functools.partial(_kernel, (rows, depth, vloc, vreal), tuple(scratch)),
            name="head_step",
            out_shape=(jax.ShapeDtypeStruct((2, depth), F32),
                       jax.ShapeDtypeStruct((rows, depth), BF16),
                       jax.ShapeDtypeStruct((vloc, depth), F32)),
            in_specs=[vm, vm, vm, vm, hbm],
            out_specs=(vm, vm, hbm),
            scratch_shapes=list(scratch.values()),
            compiler_params=pltpu.CompilerParams(
                collective_id=0, has_side_effects=True, vmem_limit_bytes=63 * 1024 * 1024),
        )(labels.reshape(1, rows), loss_weight.reshape(1, rows), hidden, norm_gain.reshape(1, depth), w_local.T)
        loss, dh, dwt, dg = pl.pallas_call(
            _finish,
            name="head_out",
            out_shape=(jax.ShapeDtypeStruct((1, 1), F32),
                       jax.ShapeDtypeStruct((rows, depth), BF16),
                       jax.ShapeDtypeStruct((vloc, depth), F32),
                       jax.ShapeDtypeStruct((1, depth), F32)),
            in_specs=[vm, vm, hbm],
            out_specs=(vm, vm, hbm, vm),
            scratch_shapes=[pltpu.VMEM((vloc, depth), F32), pltpu.SemaphoreType.DMA((2,))],
        )(red, dh, dwt)
        return loss.reshape(1), dh, dwt.T, dg.reshape(depth)

    return jax.shard_map(
        local_step,
        mesh=mesh,
        in_specs=(P(("dp", "vp"), None), P(("dp", "vp")), P(("dp", "vp")), P(None), P(None, "vp")),
        out_specs=(P("dp"), P(("dp", "vp"), None), P("dp", "vp"), P("dp")),
        check_vma=False,
    )
```

time: 983 us -> 107 us (0.11)
  waiting for transfers between devices: 662 us -> 0 us
  blocking collectives: 259 us -> 0 us
  Pallas kernels: 0 us -> 105 us
  matrix products: 33.3 us -> 0 us
  between operations: 14.1 us -> 0.8 us
  other arithmetic: 11.6 us -> 0 us
    reduce_scatter x1 -> x0, waiting for transfers between devices: 659 us -> none  [local_step(): d_normed = lax.psum_scatter(d_part, 'vp', scatter_dimension=0, tiled=True)]
    unnamed x2 -> x0, blocking collectives: 133 us -> none
    pallas_call x0 -> x2, Pallas kernels: none -> 105 us  [the longest x1 101 us: local_step(): pl.pallas_call(functools.partial(_kernel, (rows, depth, vloc, vreal), tup...]
    pmax x1 -> x0, blocking collectives: 63.3 us -> none  [local_step(): row_max = lax.pmax(jnp.max(logits, axis=1), 'vp')]
    psum x1 -> x0, blocking collectives: 62.6 us -> none  [local_step(): target = lax.psum(jnp.sum(jnp.where(is_target, logits, 0.0), axis=1), 'vp')]
    dot_general x3 -> x0, matrix products: 33.3 us -> none  [the longest x1 12.5 us: local_step(): lax.dot_general(d_logits, w_local, (((1,), (1,)), ((), ())), preferred_el...]
  transfers between devices with their start and end apart: 2 -> 0, of which waited for: 2 -> 0; matrix products, arithmetic and copies ran while one was open for 1% -> 0% of each run, Pallas kernels for 0% -> 0%
where the time goes in v2:
time: 107 us; the launch traced here: 106 us
  Pallas kernels  105 us (98%)
    pallas_call x1, Pallas kernels, local_step(): pl.pallas_call(functools.partial(_kernel, (rows, depth, vloc, vreal), tup...  101 us
    pallas_call x1, Pallas kernels, local_step(): pl.pallas_call(_finish, name='head_out', out_shape=(jax.ShapeDtypeStruct(...  4.1 us

profile of v2, /device:TPU:0, one launch (start us, length us, event | category | flops | bytes accessed | tf_op | source)
XLA Modules:
  0.0 106.3 jit_solution(8910045589929737554)
XLA Ops:
  0.6 101.4 %head_step.1 = (f32[2,1024]{1,0:T(2,128)}, bf16[32,1024]{1,0:T(8,128)(2,1)}, f32[394,1024]{1,0:T(8,128)}) custom-call(s32[1,32]{1,0:T(1,128)} %bitcast.9, f32[1,32]{1,0:T(1,128)} %bitcast.10, bf16[32,1024]{1,0:T(8,128)(2,1)} %hid_ref.1, f32[1,1024]{1,0:T(1,128)} %bitcast.8, bf16[394,1024]{1,0:T(8,128)(2,1)} %bitcast.7), custom_call_target="tpu_custom_call" | custom-call | tf_op jit(solution)/shard_map/head_step/pallas_call | solution.py:526
  102.0 4.1 %head_out.1 = (f32[1,1]{1,0:T(1,128)}, bf16[32,1024]{1,0:T(8,128)(2,1)}, f32[394,1024]{1,0:T(8,128)}, f32[1,1024]{1,0:T(1,128)}) custom-call(f32[2,1024]{1,0:T(2,128)} %get-tuple-element.11.red_ref, bf16[32,1024]{1,0:T(8,128)(2,1)} %get-tuple-element.12.dh_ref, f32[394,1024]{1,0:T(8,128)} %get-tuple-element.13.dw_ref), custom_call_target="tpu_custom_call" | custom-call | tf_op jit(solution)/shard_map/head_out/pallas_call | solution.py:538

commit v3 on v2

v3 whole, which is shorter than its diff:
```python
import functools
import math
import math

import jax
import jax.numpy as jnp
from jax import lax
from jax.experimental import pallas as pl
from jax.experimental.pallas import tpu as pltpu
from jax.sharding import PartitionSpec as P

NORM_EPS = 1e-5
PAD_COLS = 128
CHUNKS = 4
NBLK = 512
MESH = pl.DeviceIdType.MESH
F32 = jnp.float32
BF16 = jnp.bfloat16
AROUND = (1, 3, 2)
ORDER = (
    "22314430123012012300102232110133230123012361666003626211",
    "6603536215201321052130",
)
UNIT = 16384


def _around(*dims):
    offs = [{}]
    for d in dims:
        offs = [{**o, d: t} for t in (*AROUND, 0) for o in offs]
    return [o for o in offs if any(o.values())]


def _parts(depth, k):
    tiles = depth // 128
    sizes = [tiles // 3 + (1 if i < tiles % 3 else 0) for i in range(3)]
    sizes = [sizes[(i + k) % 3] for i in range(3)]
    starts = [0, sizes[0], sizes[0] + sizes[1]]
    return tuple((a * 128, n * 128) for a, n in zip(starts, sizes))


def _rowsum(x):
    return jnp.sum(x, axis=1, keepdims=True)


def _colsum(x):
    return jnp.sum(x, axis=0, keepdims=True)


def _scratch(rows, depth, vloc):
    r = rows // CHUNKS
    v = pltpu.VMEM
    c = CHUNKS
    s = {
        "xs": v((c, 4, 4, 4, r, depth), BF16),
        "acts": v((c, 4, 4, 4 * r, depth), BF16),
        "meta": v((4, 4, 4, 2, 128), F32),
        "win": v((vloc, depth), BF16),
        "w2": v((2, NBLK, depth), BF16),
        "ex": v((c, 2, 4, 4, 4, r, NBLK), F32),
        "dz": v((c, 2, 4, 4, 4 * r, NBLK), BF16),
        "gp": v((c, 4, 4, 4, r, depth), F32),
        "dwp": v((2, NBLK, depth), F32),
        "dwrx": v((NBLK, depth), F32),
        "dwo": v((vloc, depth), F32),
        "labc": v((c, 4, 4, 4 * r, 1), F32),
        "wtc": v((c, 4, 4, 4 * r, 1), F32),
        "rcol": v((c, 4, 4, 4 * r, 1), F32),
        "frow": v((c, 4, 1, 128), F32),
        "lrow": v((c, 4, 1, 128), F32),
        "stat": v((c, 3, 4, 1, 128), F32),
        "mloc": v((c, 4, 1, 128), F32),
        "statrx": v((c, 18, 4, 1, 128), F32),
        "ssum": v((2, 2, 128), F32),
        "dgacc": v((r, depth), F32),
        "redbuf": v((4, 1, depth + 256), F32),
        "redrx": v((19, 1, depth + 256), F32),
        "acct": v((4 * r, NBLK), F32),
        "accl": v((4 * r, 128), F32),
        "rx3": v((c, 3, r, depth), F32),
        "dum": v((64, UNIT // 2 // depth, depth), BF16),
        "dum1": v((128, 2, 128), F32),
        "hidv": v((rows, depth), BF16),
        "labv": v((1, rows), jnp.int32),
        "wtv": v((1, rows), F32),
        "gainv": v((1, depth), F32),
    }
    for k in range(c):
        for p, (_, w) in enumerate(_parts(depth, k)):
            shape = (2, 4) if p == 1 else (4, 2)
            s[f"rx1_{k}_{p}"] = v((6, *shape, r, w), F32)
            s[f"rx2_{k}_{p}"] = v((15, r, w) if k == c - 1 else (6, 2, r, w), F32)
    n = 96
    s["send_sem"] = pltpu.SemaphoreType.DMA((n,))
    s["recv_sem"] = pltpu.SemaphoreType.DMA((n,))
    s["loc_sem"] = pltpu.SemaphoreType.DMA((6,))
    return s


def _pick(pairs):
    return tuple(pairs.get(d, slice(None)) for d in (2, 1, 0))


def _interleave(procs):
    for i in map(int, "".join(ORDER)):
        next(procs[i], None)
    for p in procs:
        next(p, None)


def _kernel(dims, names, lab_ref, wt_ref, hid_in, gain_in, w_ref, red_ref, dh_ref, dw_ref, *refs):
    rows, depth, vloc, vreal = dims
    s = dict(zip(names, refs))
    r8 = rows // CHUNKS
    r32 = 4 * r8
    xs, acts, meta, w2, ex, dz, gp = (s[n] for n in ("xs", "acts", "meta", "w2", "ex", "dz", "gp"))
    dwp, stat, statrx, ssum = s["dwp"], s["stat"], s["statrx"], s["ssum"]
    me = lax.axis_index("vp")
    core = lax.rem(me, 2)
    chip = me // 2
    pos = (lax.rem(chip, 4), lax.rem(chip // 4, 4), chip // 16)
    stride = (2, 8, 32)
    other = me + 1 - 2 * core
    own = {0: pos[0], 1: pos[1], 2: pos[2]}
    h0, h1 = slice(0, 2), slice(2, 4)

    def at(d, step):
        return lax.rem(pos[d] + step, 4)

    def peer(off):
        return me + sum((at(d, t) - pos[d]) * stride[d] for d, t in off.items())

    groups = []

    class Group:
        def __init__(self):
            self.sems = s["send_sem"].at[len(groups)], s["recv_sem"].at[len(groups)]
            self.size, self.copies, self.got, self.sent = 0, [], False, False
            groups.append(self)

        def add(self, src, dst, device):
            c = pltpu.make_async_remote_copy(
                src_ref=src, dst_ref=dst, send_sem=self.sems[0], recv_sem=self.sems[1],
                device_id={"vp": device}, device_id_type=MESH)
            c.start()
            self.size += math.prod(src.shape) * src.dtype.itemsize
            self.copies.append(c)
            return self

        def _all(self, sem):
            ref = s["dum"] if self.size % UNIT == 0 else s["dum1"]
            unit = math.prod(ref.shape[1:]) * ref.dtype.itemsize
            part = ref.at[pl.ds(0, self.size // unit)]
            return pltpu.make_async_copy(part, part, sem)

        def wait_recv(self):
            self.got = True
            if len(self.copies) == 1:
                self.copies[0].wait_recv()
            else:
                self._all(self.sems[1]).wait()

        def wait_send(self):
            if self.sent:
                return
            self.sent = True
            if len(self.copies) == 1:
                self.copies[0].wait_send()
            else:
                self._all(self.sems[0]).wait()

    def copy(src, dst, device):
        return Group().add(src, dst, device)

    barrier = pltpu.get_barrier_semaphore()
    peers = [peer(o) for d in range(3) for o in _around(d)] + [other]
    for p in peers:
        pl.semaphore_signal(barrier, inc=1, device_id={"vp": p}, device_id_type=MESH)
    hid_ref, lab_v, wt_v, gain_v = (s[n] for n in ("hidv", "labv", "wtv", "gainv"))
    loads = [pltpu.make_async_copy(a, b, s["loc_sem"].at[i]) for i, (a, b) in enumerate(
        ((hid_in, hid_ref), (lab_ref, lab_v), (wt_ref, wt_v), (gain_in, gain_v), (w_ref, s["win"])))]
    for c in loads:
        c.start()
    wload = loads.pop()
    for n in ("dgacc", "acct", "accl"):
        s[n][...] = jnp.zeros_like(s[n])
    for c in loads:
        c.wait()

    for k in range(CHUNKS):
        xs[k, pos[2], pos[1], pos[0]] = hid_ref[k * r8:(k + 1) * r8, :]
    mine = meta.at[pos[2], pos[1], pos[0]]
    mine[...] = jnp.zeros((2, 128), F32)
    mine[0:1, 0:rows] = lab_v[...].astype(F32)
    mine[1:2, 0:rows] = wt_v[...]
    gain = gain_v[...]
    pl.semaphore_wait(barrier, len(peers))

    lane = lax.broadcasted_iota(jnp.int32, (r32, 128), 1)
    row = lax.broadcasted_iota(jnp.int32, (r32, 128), 0)
    lane_n = lax.broadcasted_iota(jnp.int32, (r32, NBLK), 1)
    bases = [(2 * chip + b) * vloc for b in range(2)]
    shared = {}

    def mview(pairs):
        return meta.at[_pick(pairs)]

    def order(p):
        return p, (p + 1) % 3, (p + 2) % 3

    def half_mat(fn):
        lax.fori_loop(0, 2, lambda i, _: (fn(i), 0)[1], 0)

    def w_proc():
        yield
        wload.wait()
        w2[core, 0:vloc, :] = s["win"][...]
        w2[core, vloc:, :] = jnp.zeros((NBLK - vloc, depth), BF16)
        shared["w"] = copy(w2.at[core], w2.at[core], other)
        yield

    def chunk(k):
        parts = _parts(depth, k)
        last = k == CHUNKS - 1

        def xsl(c, pairs):
            return xs.at[(k, *_pick(pairs), slice(None), pl.ds(*c))]

        def spread(group, view, pairs, dims, src=None):
            ref = view(pairs) if src is None else src
            for o in _around(*dims):
                group.add(ref, view(pairs), peer(o))

        def views(p):
            return [functools.partial(xsl, parts[p])] + [mview] * (p + k == 0)

        def fresh():
            flight[:] = [Group() for _ in range(1 if k else 2)]
            return flight

        def settle():
            for cp in flight:
                cp.wait_recv()

        flight = []
        if k:
            yield
        fresh()
        for p, c in enumerate(parts):
            dims = order(p)[:1]
            spread(flight[0], views(p)[0], own, dims, hid_ref.at[pl.ds(k * r8, r8), pl.ds(*c)])
            for vw in views(p)[1:]:
                spread(flight[1], vw, own, dims)
        yield
        settle()
        fresh()
        for p in range(3):
            _, d, d2 = order(p)
            for i, vw in enumerate(views(p)):
                spread(flight[i], vw, {d: pos[d], d2: pos[d2]}, (d,))
        yield
        settle()
        if k:
            ring = [Group(), Group()]
        else:
            fresh()
        for p in range(3):
            _, _, d = order(p)
            for i, vw in enumerate(views(p)):
                if k == 0:
                    spread(flight[i], vw, {d: pos[d]}, (d,))
                else:
                    src = vw({d: pos[d]})
                    for g, t in zip(ring, (1, 3)):
                        g.add(src, src, peer({d: t}))
        yield
        if k:
            fresh()
            for g, t, h in zip(ring, (1, 3), (h0, h1)):
                g.wait_recv()
                for p, c in enumerate(parts):
                    d0, _, d = order(p)
                    vv = xsl(c, {d: at(d, 4 - t), d0: h})
                    flight[0].add(vv, vv, peer({d: t}))
        if k:
            yield
        settle()

        def norm(z, _):
            for y in range(4):
                x = xs[k, z, y].astype(F32).reshape(r32, depth)
                inv = lax.rsqrt(jnp.mean(x * x, axis=-1, keepdims=True) + NORM_EPS)
                s["rcol"][k, z, y] = inv
                acts[k, z, y] = (x * inv * gain).astype(BF16)
            return 0

        lax.fori_loop(0, 4, norm, 0)
        if k == 0:
            ssum[0] = jnp.sum(meta[...].reshape(64, 2, 128), axis=0)
            shared["s"] = copy(ssum.at[0], ssum.at[1], other)
            shared["w"].wait_recv()
        yield

        def zdot(i):
            a = acts[k, pl.ds(2 * i, 2)].reshape(8 * r32, depth)
            for b in range(2):
                ex[k, b, pl.ds(2 * i, 2)] = lax.dot_general(
                    a, w2[b], (((1,), (1,)), ((), ())),
                    preferred_element_type=F32).reshape(2, 4, 4, r8, NBLK)

        half_mat(zdot)
        yield

        def soft(z, _):
            mrow = jnp.zeros((1, 128), F32)
            srow = jnp.zeros((1, 128), F32)
            for y in range(4):
                def col(j):
                    m = jnp.broadcast_to(meta[z, y, :, j:j + 1, :], (4, r8, 128)).reshape(r32, 128)
                    return _rowsum(jnp.where(lane == k * r8 + lax.rem(row, r8), m, 0.0))

                lab, wt = col(0), col(1)
                s["labc"][k, z, y] = lab
                s["wtc"][k, z, y] = wt
                labi = lab.astype(jnp.int32)
                vals = []
                tgt = jnp.zeros((r32, NBLK), F32)
                for b in range(2):
                    val = ex[k, b, z, y].reshape(r32, NBLK)
                    ok = (lane_n < vloc) & (lane_n < vreal - bases[b])
                    tgt = tgt + jnp.where((lane_n == labi - bases[b]) & (lane_n < vloc), val, 0.0)
                    vals.append(jnp.where(ok, val, -jnp.inf))
                mx = jnp.max(jnp.maximum(vals[0], vals[1]), axis=1, keepdims=True)
                es = [jnp.exp(val - mx) for val in vals]
                sm = _rowsum(es[0] + es[1])
                for b in range(2):
                    ex[k, b, z, y] = es[b].reshape(4, r8, NBLK)
                here = lane == row + r32 * y
                mrow = mrow + _colsum(jnp.where(here, mx, 0.0))
                srow = srow + _colsum(jnp.where(here, sm, 0.0))
                s["acct"][...] += tgt * wt
            s["mloc"][k, z] = mrow
            stat[k, 0, z] = mrow + jnp.log(srow)
            return 0

        lax.fori_loop(0, 4, soft, 0)
        for i, dims in enumerate(((0, 1), (2,))):
            offs = _around(*dims)
            rx = statrx.at[k, pl.ds(15 * i, len(offs))]
            g = Group()
            for j, o in enumerate(offs):
                g.add(stat.at[k, i], rx.at[j], peer(o))
            yield
            g.wait_recv()
            mine = stat[k, i]
            got = rx[...]
            top = jnp.maximum(mine, jnp.max(got, axis=0))
            stat[k, i + 1] = top + jnp.log(jnp.exp(mine - top) + jnp.sum(jnp.exp(got - top), axis=0))
        lse = stat[k, 2]
        s["lrow"][k] = lse
        s["frow"][k] = jnp.exp(s["mloc"][k] - lse)
        if k == 0:
            shared["s"].wait_recv()
        total_w = _rowsum(ssum[0, 1:] + ssum[1, 1:])

        def grad(z, _):
            for y in range(4):
                here = lane == row + r32 * y
                fr = jnp.broadcast_to(s["frow"][k, z], (r32, 128))
                lr = jnp.broadcast_to(s["lrow"][k, z], (r32, 128))
                fc = _rowsum(jnp.where(here, fr, 0.0))
                lab = s["labc"][k, z, y].astype(jnp.int32)
                sc = s["wtc"][k, z, y] / total_w
                s["accl"][...] += jnp.where(here, lr, 0.0) * sc
                for b in range(2):
                    prob = ex[k, b, z, y].reshape(r32, NBLK) * fc
                    hit = (lane_n == lab - bases[b]) & (lane_n < vloc)
                    dz[k, b, z, y] = ((prob - jnp.where(hit, 1.0, 0.0)) * sc).astype(BF16)
            return 0

        lax.fori_loop(0, 4, grad, 0)

        def gdot(i):
            zz = pl.ds(2 * i, 2)
            g = jnp.dot(dz[k, 0, zz].reshape(8 * r32, NBLK), w2[0], preferred_element_type=F32)
            g = g + jnp.dot(dz[k, 1, zz].reshape(8 * r32, NBLK), w2[1], preferred_element_type=F32)
            gp[k, zz] = g.reshape(2, 4, 4, r8, depth)

        half_mat(gdot)

        def gsl(c, pairs):
            return gp.at[(k, *_pick(pairs), slice(None), pl.ds(*c))]

        def rs_far(bufs, c, d, hd, base, gs):
            for i, (g, h, t) in enumerate(zip(gs, (h0, h1), (1, 3))):
                g.add(gsl(c, {**base, d: at(d, 2), hd: h}), bufs.at[i], peer({d: t}))

        def rs_near(bufs, c, d, hd, base, gs):
            for i, (h, t) in enumerate(zip((h1, h0), (1, 3))):
                gs[2].add(gsl(c, {**base, d: at(d, t), hd: h}), bufs.at[2 + i], peer({d: t}))

        def triple():
            return [Group() for _ in range(3)]

        def each(hd, rest, half, fixed, fn):
            if rest is None:
                for i in range(2):
                    fn((i,), {**fixed, hd: 2 * half + i})
                return

            def body(t, _):
                i, j = t // 4, lax.rem(t, 4)
                fn((i, j) if hd > rest else (j, i), {**fixed, hd: 2 * half + i, rest: j})
                return 0

            lax.fori_loop(0, 8, body, 0)

        def rs_relay(todo, gs):
            for i, t in enumerate((1, 3)):
                gs[i].wait_recv()
                for bufs, c, d, hd, rest, base in todo:
                    def add(idx, pairs):
                        bufs[(i, *idx)] += gp[(k, *_pick(pairs), slice(None), pl.ds(*c))]

                    each(hd, rest, i, {**base, d: at(d, t)}, add)
                    gs[2].add(bufs.at[i], bufs.at[4 + i], peer({d: t}))

        def rs_finish(bufs, c, d, hd, rest, base):
            for half, (k1, k2) in enumerate(((3, 4), (2, 5))):
                def add(idx, pairs):
                    sl = (k, *_pick(pairs), slice(None), pl.ds(*c))
                    gp[sl] = gp[sl] + (bufs[(k1, *idx)] + bufs[(k2, *idx)])

                each(hd, rest, half, {**base, d: pos[d]}, add)

        rx1 = [s[f"rx1_{k}_{p}"] for p in range(3)]
        rx2 = [s[f"rx2_{k}_{p}"] for p in range(3)]
        todo1 = [(rx1[p], c, *order(p), {}) for p, c in enumerate(parts)]
        todo2 = [(rx2[p], c, order(p)[1], order(p)[2], None, {p: pos[p]}) for p, c in enumerate(parts)]
        gs1 = triple()
        for bufs, c, d, hd, _, base in todo1:
            rs_far(bufs, c, d, hd, base, gs1)
        yield
        for bufs, c, d, hd, _, base in todo1:
            rs_near(bufs, c, d, hd, base, gs1)
        yield

        def dg(z, _):
            acc = jnp.zeros((r8, depth), F32)
            for y in range(4):
                n = xs[k, z, y].astype(F32).reshape(r32, depth) * s["rcol"][k, z, y]
                t = gp[k, z, y].reshape(r32, depth) * n
                acc = acc + jnp.sum(t.reshape(4, r8, depth), axis=0)
            s["dgacc"][...] += acc
            return 0

        lax.fori_loop(0, 4, dg, 0)
        yield
        rs_relay(todo1, gs1)
        yield
        gs1[2].wait_recv()
        gs2 = [Group()] if last else triple()
        for t1, (bufs, c, d, hd, _, base) in zip(todo1, todo2):
            rs_finish(*t1)
            if last:
                for i, o in enumerate(_around(d, hd)):
                    gs2[0].add(gsl(c, {**base, **{e: at(e, o[e]) for e in o}}), bufs.at[i], peer(o))
            else:
                rs_far(bufs, c, d, hd, base, gs2)
                rs_near(bufs, c, d, hd, base, gs2)
        yield
        if last:
            for g in groups:
                if g.got:
                    g.wait_send()
            gs2[0].wait_recv()
            for bufs, c, *_ in todo2:
                s["rx3"][k, 0, :, pl.ds(*c)] = jnp.sum(bufs[...], axis=0)
        else:
            rs_relay(todo2, gs2)
            yield
            gs2[2].wait_recv()
            g3 = Group()
            for t2 in todo2:
                rs_finish(*t2)
                _, c, d1, d, _, base = t2
                for i, t in enumerate(AROUND):
                    g3.add(gsl(c, {**base, d1: pos[d1], d: at(d, t)}), s["rx3"].at[k, i, :, pl.ds(*c)], peer({d: t}))
            yield
            g3.wait_recv()
        g = gp[k, pos[2], pos[1], pos[0]]
        for i in range(1 if last else 3):
            g = g + s["rx3"][k, i]
        x = hid_ref[k * r8:(k + 1) * r8, :].astype(F32)
        inv = lax.rsqrt(jnp.mean(x * x, axis=-1, keepdims=True) + NORM_EPS)
        n = x * inv
        u = g * gain
        dh_ref[k * r8:(k + 1) * r8, :] = (inv * (u - n * jnp.mean(u * n, axis=-1, keepdims=True))).astype(BF16)
        yield

    def dw_proc():
        for first in (True, False):
            blk = 1 - core if first else core
            for k in range(CHUNKS):
                def part():
                    return lax.dot_general(dz[k, blk].reshape(16 * r32, NBLK), acts[k].reshape(16 * r32, depth),
                                           (((0,), (0,)), ((), ())), preferred_element_type=F32)

                if k == 0:
                    dwp[blk] = part()
                else:
                    dwp[blk] += part()
                if k < CHUNKS - 1:
                    yield
            if first:
                cp = copy(dwp.at[blk], s["dwrx"], other)
            yield
        cp.wait_recv()
        s["dwo"][...] = dwp[core, 0:vloc, :] + s["dwrx"][0:vloc, :]
        shared["o"] = pltpu.make_async_copy(s["dwo"], dw_ref, s["loc_sem"].at[5])
        shared["o"].start()
        yield

    def red_proc():
        redbuf, redrx = s["redbuf"], s["redrx"]
        total_w = _rowsum(ssum[0, 1:] + ssum[1, 1:])
        redbuf[0, :, :depth] = _colsum(s["dgacc"][...])
        lsum = jnp.sum(s["accl"][...]) * (1.0 / 64.0) - jnp.sum(s["acct"][...] / total_w)
        redbuf[0, :, depth:] = jnp.broadcast_to(lsum.reshape(1, 1), (1, 256))
        cp = copy(redbuf.at[0], redrx.at[0], other)
        yield
        cp.wait_recv()
        redbuf[1] = redbuf[0] + redrx[0]
        for i, dims in enumerate(((0, 1), (2,))):
            offs = _around(*dims)
            rx = redrx.at[pl.ds(15 * i + 1, len(offs))]
            g = Group()
            for j, o in enumerate(offs):
                g.add(redbuf.at[1 + i], rx.at[j], peer(o))
            yield
            g.wait_recv()
            redbuf[2 + i] = redbuf[1 + i] + jnp.sum(rx[...], axis=0)
        red_ref[...] = redbuf[3]

    _interleave([chunk(k) for k in range(CHUNKS)] + [w_proc(), red_proc(), dw_proc()])
    shared["o"].wait()
    for c in groups:
        c.wait_send()


def _finish(red_ref, dh_ref, dw_ref, loss_out, dh_out, dw_out, dg_out, redv, dhv, buf, lossv, dgv, sem):
    step = buf.shape[1] // 4
    cols = [(slice(None), pl.ds(i * step, step)) for i in range(4)]
    moves = [(red_ref, redv, None)] + [(dw_ref.at[c], buf.at[c], dw_out.at[c]) for c in cols] + [(dh_ref, dhv, dh_out)]
    gets = [pltpu.make_async_copy(a, b, sem.at[i, 0]) for i, (a, b, _) in enumerate(moves)]
    puts = [pltpu.make_async_copy(b, c, sem.at[i, 1]) for i, (_, b, c) in enumerate(moves) if c is not None]
    for g in gets:
        g.start()
    gets[0].wait()
    lossv[...] = redv[:, dgv.shape[1]:dgv.shape[1] + 1]
    dgv[...] = redv[:, :dgv.shape[1]]
    puts += [pltpu.make_async_copy(lossv, loss_out, sem.at[0, 1]), pltpu.make_async_copy(dgv, dg_out, sem.at[6, 1])]
    for p in puts[5:]:
        p.start()
    for g, p in zip(gets[1:], puts):
        g.wait()
        p.start()
    for p in puts:
        p.wait()


def solution(mesh):
    def local_step(hidden, labels, loss_weight, norm_gain, w_local):
        rows, depth = hidden.shape
        vloc = w_local.shape[1]
        vreal = vloc * mesh.shape["vp"] - PAD_COLS
        vm = pl.BlockSpec(memory_space=pltpu.VMEM)
        hbm = pl.BlockSpec(memory_space=pl.ANY)
        scratch = _scratch(rows, depth, vloc)
        red, dh, dwt = pl.pallas_call(
            functools.partial(_kernel, (rows, depth, vloc, vreal), tuple(scratch)),
            name="head_step",
            out_shape=(jax.ShapeDtypeStruct((1, depth + 256), F32),
                       jax.ShapeDtypeStruct((rows, depth), BF16),
                       jax.ShapeDtypeStruct((vloc, depth), F32)),
            in_specs=[hbm] * 5,
            out_specs=(vm, vm, hbm),
            scratch_shapes=list(scratch.values()),
            compiler_params=pltpu.CompilerParams(
                collective_id=0, has_side_effects=True, vmem_limit_bytes=63 * 1024 * 1024),
        )(labels.reshape(1, rows), loss_weight.reshape(1, rows), hidden, norm_gain.reshape(1, depth), w_local.T)
        loss, dh, dwt, dg = pl.pallas_call(
            _finish,
            name="head_out",
            out_shape=(jax.ShapeDtypeStruct((1, 1), F32),
                       jax.ShapeDtypeStruct((rows, depth), BF16),
                       jax.ShapeDtypeStruct((vloc, depth), F32),
                       jax.ShapeDtypeStruct((1, depth), F32)),
            in_specs=[hbm] * 3,
            out_specs=[hbm] * 4,
            scratch_shapes=[pltpu.VMEM((1, depth + 256), F32), pltpu.VMEM((rows, depth), BF16),
                            pltpu.VMEM((vloc, depth), F32), pltpu.VMEM((1, 1), F32), pltpu.VMEM((1, depth), F32),
                            pltpu.SemaphoreType.DMA((7, 2))],
        )(red, dh, dwt)
        return loss.reshape(1), dh, dwt.T, dg.reshape(depth)

    return jax.shard_map(
        local_step,
        mesh=mesh,
        in_specs=(P(("dp", "vp"), None), P(("dp", "vp")), P(("dp", "vp")), P(None), P(None, "vp")),
        out_specs=(P("dp"), P(("dp", "vp"), None), P("dp", "vp"), P("dp")),
        check_vma=False,
    )
```

time: 107 us -> 82.9 us (0.77)
  Pallas kernels: 105 us -> 82.1 us
    pallas_call x1, Pallas kernels: 101 us -> 79.7 us  [local_step(): pl.pallas_call(functools.partial(_kernel, (rows, depth, vloc, vreal), tup...]
    pallas_call x1, Pallas kernels: 4.1 us -> 2.31 us  [local_step(): pl.pallas_call(_finish, name='head_out', out_shape=(jax.ShapeDtypeStruct(...]
where the time goes in v3:
time: 82.9 us; the launch traced here: 82.7 us
  Pallas kernels  82.1 us (99%)
    pallas_call x1, Pallas kernels, local_step(): pl.pallas_call(functools.partial(_kernel, (rows, depth, vloc, vreal), tup...  79.7 us
    pallas_call x1, Pallas kernels, local_step(): pl.pallas_call(_finish, name='head_out', out_shape=(jax.ShapeDtypeStruct(...  2.31 us

profile of v3, /device:TPU:0, one launch (start us, length us, event | category | flops | bytes accessed | tf_op | source)
XLA Modules:
  0.0 82.7 jit_solution(3204555391909783464)
XLA Ops:
  0.6 79.7 %head_step.1 = (f32[1,1280]{1,0:T(1,128)}, bf16[32,1024]{1,0:T(8,128)(2,1)}, f32[394,1024]{1,0:T(8,128)}) custom-call(s32[1,32]{1,0:T(1,128)} %bitcast.9, f32[1,32]{1,0:T(1,128)} %bitcast.10, bf16[32,1024]{1,0:T(8,128)(2,1)} %hid_in.1, f32[1,1024]{1,0:T(1,128)} %bitcast.8, bf16[394,1024]{1,0:T(8,128)(2,1)} %bitcast.7), custom_call_target="tpu_custom_call" | custom-call | tf_op jit(solution)/shard_map/head_step/pallas_call | solution.py:580
  80.4 2.3 %head_out.1 = (f32[1,1]{1,0:T(1,128)}, bf16[32,1024]{1,0:T(8,128)(2,1)}, f32[394,1024]{1,0:T(8,128)}, f32[1,1024]{1,0:T(1,128)}) custom-call(f32[1,1280]{1,0:T(1,128)} %get-tuple-element.11.red_ref, bf16[32,1024]{1,0:T(8,128)(2,1)} %get-tuple-element.12.dh_ref, f32[394,1024]{1,0:T(8,128)} %get-tuple-element.13.dw_ref), custom_call_target="tpu_custom_call" | custom-call | tf_op jit(solution)/shard_map/head_out/pallas_call | solution.py:592

commit v4 on v3

--- a/solution.py
+++ b/solution.py
@@ -18,10 +18,11 @@
 BF16 = jnp.bfloat16
 AROUND = (1, 3, 2)
 ORDER = (
-    "22314430123012012300102232110133230123012361666003626211",
-    "6603536215201321052130",
+    "04242133103120210000322221111033233102310236616666002636",
+    "621135320153012530123012",
 )
 UNIT = 16384
+DIRECT = (0, 1, 2, 3)
 
 
 def _around(*dims):
@@ -89,7 +90,7 @@
         for p, (_, w) in enumerate(_parts(depth, k)):
             shape = (2, 4) if p == 1 else (4, 2)
             s[f"rx1_{k}_{p}"] = v((6, *shape, r, w), F32)
-            s[f"rx2_{k}_{p}"] = v((15, r, w) if k == c - 1 else (6, 2, r, w), F32)
+            s[f"rx2_{k}_{p}"] = v((3, 4, r, w) if k == c - 1 else (6, 2, r, w), F32)
     n = 96
     s["send_sem"] = pltpu.SemaphoreType.DMA((n,))
     s["recv_sem"] = pltpu.SemaphoreType.DMA((n,))
@@ -260,21 +261,22 @@
                 spread(flight[i], vw, {d: pos[d], d2: pos[d2]}, (d,))
         yield
         settle()
-        if k:
+        direct = k in DIRECT
+        if not direct:
             ring = [Group(), Group()]
         else:
             fresh()
         for p in range(3):
             _, _, d = order(p)
             for i, vw in enumerate(views(p)):
-                if k == 0:
+                if direct:
                     spread(flight[i], vw, {d: pos[d]}, (d,))
                 else:
                     src = vw({d: pos[d]})
                     for g, t in zip(ring, (1, 3)):
                         g.add(src, src, peer({d: t}))
         yield
-        if k:
+        if not direct:
             fresh()
             for g, t, h in zip(ring, (1, 3), (h0, h1)):
                 g.wait_recv()
@@ -282,7 +284,7 @@
                     d0, _, d = order(p)
                     vv = xsl(c, {d: at(d, 4 - t), d0: h})
                     flight[0].add(vv, vv, peer({d: t}))
-        if k:
+        if not direct:
             yield
         settle()
 
@@ -308,7 +310,7 @@
                     a, w2[b], (((1,), (1,)), ((), ())),
                     preferred_element_type=F32).reshape(2, 4, 4, r8, NBLK)
 
-        half_mat(zdot)
+        zdot(0)
         yield
 
         def soft(z, _):
@@ -343,7 +345,12 @@
             stat[k, 0, z] = mrow + jnp.log(srow)
             return 0
 
-        lax.fori_loop(0, 4, soft, 0)
+        zdot(1)
+        soft(0, 0)
+        soft(1, 0)
+        yield
+        soft(2, 0)
+        soft(3, 0)
         for i, dims in enumerate(((0, 1), (2,))):
             offs = _around(*dims)
             rx = statrx.at[k, pl.ds(15 * i, len(offs))]
@@ -378,7 +385,6 @@
                     dz[k, b, z, y] = ((prob - jnp.where(hit, 1.0, 0.0)) * sc).astype(BF16)
             return 0
 
-        lax.fori_loop(0, 4, grad, 0)
 
         def gdot(i):
             zz = pl.ds(2 * i, 2)
@@ -386,7 +392,10 @@
             g = g + jnp.dot(dz[k, 1, zz].reshape(8 * r32, NBLK), w2[1], preferred_element_type=F32)
             gp[k, zz] = g.reshape(2, 4, 4, r8, depth)
 
-        half_mat(gdot)
+        for i in range(2):
+            grad(2 * i, 0)
+            grad(2 * i + 1, 0)
+            gdot(i)
 
         def gsl(c, pairs):
             return gp.at[(k, *_pick(pairs), slice(None), pl.ds(*c))]
@@ -402,36 +411,17 @@
         def triple():
             return [Group() for _ in range(3)]
 
-        def each(hd, rest, half, fixed, fn):
-            if rest is None:
-                for i in range(2):
-                    fn((i,), {**fixed, hd: 2 * half + i})
-                return
-
-            def body(t, _):
-                i, j = t // 4, lax.rem(t, 4)
-                fn((i, j) if hd > rest else (j, i), {**fixed, hd: 2 * half + i, rest: j})
-                return 0
-
-            lax.fori_loop(0, 8, body, 0)
-
         def rs_relay(todo, gs):
             for i, t in enumerate((1, 3)):
                 gs[i].wait_recv()
-                for bufs, c, d, hd, rest, base in todo:
-                    def add(idx, pairs):
-                        bufs[(i, *idx)] += gp[(k, *_pick(pairs), slice(None), pl.ds(*c))]
-
-                    each(hd, rest, i, {**base, d: at(d, t)}, add)
+                for bufs, c, d, hd, _, base in todo:
+                    bufs[i] += gp[(k, *_pick({**base, d: at(d, t), hd: (h0, h1)[i]}), slice(None), pl.ds(*c))]
                     gs[2].add(bufs.at[i], bufs.at[4 + i], peer({d: t}))
 
-        def rs_finish(bufs, c, d, hd, rest, base):
-            for half, (k1, k2) in enumerate(((3, 4), (2, 5))):
-                def add(idx, pairs):
-                    sl = (k, *_pick(pairs), slice(None), pl.ds(*c))
-                    gp[sl] = gp[sl] + (bufs[(k1, *idx)] + bufs[(k2, *idx)])
-
-                each(hd, rest, half, {**base, d: pos[d]}, add)
+        def rs_finish(bufs, c, d, hd, _, base):
+            for h, k1, k2 in ((h0, 3, 4), (h1, 2, 5)):
+                sl = (k, *_pick({**base, d: pos[d], hd: h}), slice(None), pl.ds(*c))
+                gp[sl] = gp[sl] + (bufs[k1] + bufs[k2])
 
         rx1 = [s[f"rx1_{k}_{p}"] for p in range(3)]
         rx2 = [s[f"rx2_{k}_{p}"] for p in range(3)]
@@ -463,33 +453,35 @@
         for t1, (bufs, c, d, hd, _, base) in zip(todo1, todo2):
             rs_finish(*t1)
             if last:
-                for i, o in enumerate(_around(d, hd)):
-                    gs2[0].add(gsl(c, {**base, **{e: at(e, o[e]) for e in o}}), bufs.at[i], peer(o))
+                for i, t in enumerate(AROUND):
+                    gs2[0].add(gsl(c, {**base, d: at(d, t)}), bufs.at[i], peer({d: t}))
             else:
                 rs_far(bufs, c, d, hd, base, gs2)
                 rs_near(bufs, c, d, hd, base, gs2)
+        yield
+        if last:
+            gs2[0].wait_recv()
+            for bufs, c, d, _, _, base in todo2:
+                sl = (k, *_pick({**base, d: pos[d]}), slice(None), pl.ds(*c))
+                gp[sl] = (gp[sl] + bufs[0]) + (bufs[1] + bufs[2])
+        else:
+            rs_relay(todo2, gs2)
+            yield
+            gs2[2].wait_recv()
+            for t2 in todo2:
+                rs_finish(*t2)
+        g3 = Group()
+        for _, c, d1, d, _, base in todo2:
+            for i, t in enumerate(AROUND):
+                g3.add(gsl(c, {**base, d1: pos[d1], d: at(d, t)}), s["rx3"].at[k, i, :, pl.ds(*c)], peer({d: t}))
         yield
         if last:
             for g in groups:
                 if g.got:
                     g.wait_send()
-            gs2[0].wait_recv()
-            for bufs, c, *_ in todo2:
-                s["rx3"][k, 0, :, pl.ds(*c)] = jnp.sum(bufs[...], axis=0)
-        else:
-            rs_relay(todo2, gs2)
-            yield
-            gs2[2].wait_recv()
-            g3 = Group()
-            for t2 in todo2:
-                rs_finish(*t2)
-                _, c, d1, d, _, base = t2
-                for i, t in enumerate(AROUND):
-                    g3.add(gsl(c, {**base, d1: pos[d1], d: at(d, t)}), s["rx3"].at[k, i, :, pl.ds(*c)], peer({d: t}))
-            yield
-            g3.wait_recv()
+        g3.wait_recv()
         g = gp[k, pos[2], pos[1], pos[0]]
-        for i in range(1 if last else 3):
+        for i in range(3):
             g = g + s["rx3"][k, i]
         x = hid_ref[k * r8:(k + 1) * r8, :].astype(F32)
         inv = lax.rsqrt(jnp.mean(x * x, axis=-1, keepdims=True) + NORM_EPS)

time: 82.9 us -> 79.5 us (0.959)
  Pallas kernels: 82.1 us -> 78.3 us
    pallas_call x1, Pallas kernels: 79.7 us -> 76 us  [local_step(): pl.pallas_call(functools.partial(_kernel, (rows, depth, vloc, vreal), tup...]
where the time goes in v4:
time: 79.5 us; the launch traced here: 79.1 us
  Pallas kernels  78.3 us (98%)
  between operations  0.8 us (1%)
    pallas_call x1, Pallas kernels, local_step(): pl.pallas_call(functools.partial(_kernel, (rows, depth, vloc, vreal), tup...  76 us
    pallas_call x1, Pallas kernels, local_step(): pl.pallas_call(_finish, name='head_out', out_shape=(jax.ShapeDtypeStruct(...  2.31 us

profile of v4, /device:TPU:0, one launch (start us, length us, event | category | flops | bytes accessed | tf_op | source)
XLA Modules:
  0.0 79.1 jit_solution(17392333420238915488)
XLA Ops:
  0.6 76.0 %head_step.1 = (f32[1,1280]{1,0:T(1,128)}, bf16[32,1024]{1,0:T(8,128)(2,1)}, f32[394,1024]{1,0:T(8,128)}) custom-call(s32[1,32]{1,0:T(1,128)} %bitcast.9, f32[1,32]{1,0:T(1,128)} %bitcast.10, bf16[32,1024]{1,0:T(8,128)(2,1)} %hid_in.1, f32[1,1024]{1,0:T(1,128)} %bitcast.8, bf16[394,1024]{1,0:T(8,128)(2,1)} %bitcast.7), custom_call_target="tpu_custom_call" | custom-call | tf_op jit(solution)/shard_map/head_step/pallas_call | solution.py:572
  76.6 2.3 %head_out.1 = (f32[1,1]{1,0:T(1,128)}, bf16[32,1024]{1,0:T(8,128)(2,1)}, f32[394,1024]{1,0:T(8,128)}, f32[1,1024]{1,0:T(1,128)}) custom-call(f32[1,1280]{1,0:T(1,128)} %get-tuple-element.11.red_ref, bf16[32,1024]{1,0:T(8,128)(2,1)} %get-tuple-element.12.dh_ref, f32[394,1024]{1,0:T(8,128)} %get-tuple-element.13.dw_ref), custom_call_target="tpu_custom_call" | custom-call | tf_op jit(solution)/shard_map/head_out/pallas_call | solution.py:584

commit v5 on v4

--- a/solution.py
+++ b/solution.py
@@ -18,8 +18,8 @@
 BF16 = jnp.bfloat16
 AROUND = (1, 3, 2)
 ORDER = (
-    "04242133103120210000322221111033233102310236616666002636",
-    "621135320153012530123012",
+    "01342423101230210000322221110133233012301366206166360626",
+    "261135320153201532013201",
 )
 UNIT = 16384
 DIRECT = (0, 1, 2, 3)
@@ -296,7 +296,8 @@
                 acts[k, z, y] = (x * inv * gain).astype(BF16)
             return 0
 
-        lax.fori_loop(0, 4, norm, 0)
+        norm(0, 0)
+        norm(1, 0)
         if k == 0:
             ssum[0] = jnp.sum(meta[...].reshape(64, 2, 128), axis=0)
             shared["s"] = copy(ssum.at[0], ssum.at[1], other)
@@ -311,6 +312,8 @@
                     preferred_element_type=F32).reshape(2, 4, 4, r8, NBLK)
 
         zdot(0)
+        norm(2, 0)
+        norm(3, 0)
         yield
 
         def soft(z, _):

time: 79.5 us -> 79 us (level)
  no operation moved by 1% of the time
where the time goes in v5:
time: 79 us; the launch traced here: 78.9 us
  Pallas kernels  78.1 us (99%)
  between operations  0.8 us (1%)
    pallas_call x1, Pallas kernels, local_step(): pl.pallas_call(functools.partial(_kernel, (rows, depth, vloc, vreal), tup...  75.8 us
    pallas_call x1, Pallas kernels, local_step(): pl.pallas_call(_finish, name='head_out', out_shape=(jax.ShapeDtypeStruct(...  2.31 us

profile of v5, /device:TPU:0, one launch (start us, length us, event | category | flops | bytes accessed | tf_op | source)
XLA Modules:
  0.0 78.9 jit_solution(11868893052407355036)
XLA Ops:
  0.6 75.8 %head_step.1 = (f32[1,1280]{1,0:T(1,128)}, bf16[32,1024]{1,0:T(8,128)(2,1)}, f32[394,1024]{1,0:T(8,128)}) custom-call(s32[1,32]{1,0:T(1,128)} %bitcast.9, f32[1,32]{1,0:T(1,128)} %bitcast.10, bf16[32,1024]{1,0:T(8,128)(2,1)} %hid_in.1, f32[1,1024]{1,0:T(1,128)} %bitcast.8, bf16[394,1024]{1,0:T(8,128)(2,1)} %bitcast.7), custom_call_target="tpu_custom_call" | custom-call | tf_op jit(solution)/shard_map/head_step/pallas_call | solution.py:575
  76.4 2.3 %head_out.1 = (f32[1,1]{1,0:T(1,128)}, bf16[32,1024]{1,0:T(8,128)(2,1)}, f32[394,1024]{1,0:T(8,128)}, f32[1,1024]{1,0:T(1,128)}) custom-call(f32[1,1280]{1,0:T(1,128)} %get-tuple-element.11.red_ref, bf16[32,1024]{1,0:T(8,128)(2,1)} %get-tuple-element.12.dh_ref, f32[394,1024]{1,0:T(8,128)} %get-tuple-element.13.dw_ref), custom_call_target="tpu_custom_call" | custom-call | tf_op jit(solution)/shard_map/head_out/pallas_call | solution.py:587
